TPU v7x, 32 devices: a whole 2x2x4 slice. The times are simulated.
32 devices in a mesh: dp: 2 (over x), tp: 4 (over z), sp: 4 (over y, core).
Axes of the slice: x: 2, y: 2, z: 4, core: 2. Of those that a mesh axis runs over, the one named last changes fastest.
Arguments:
- x_in: bfloat16 [8192, 4096], P(('dp', 'sp'), 'tp'), parts along dimension 0
- w_qkv: bfloat16 [4096, 12288], P('sp', 'tp')
- w_out: bfloat16 [4096, 4096], P('sp', 'tp')
- seg_ids: int32 [8192], P(('dp', 'sp')), parts along dimension 0
Outputs:
- output: bfloat16 [8192, 4096], P(('dp', 'sp'), 'tp'), parts along dimension 0
There are 2 independent parts. A program takes and returns all parts, laid end to end along the dimension named above; an argument that names none is the same for every part.
All inputs are finite; a program needn't handle non-finite values.
Results may differ from a plain program's by a relative error of at most 0.00336.
Values are sent between devices in bfloat16 or wider.
A program may use at most 1 GiB of HBM per device.

v0:
```python
import jax
import jax.numpy as jnp
from jax import lax
from jax.sharding import PartitionSpec as P, NamedSharding

HEAD_DIM = 128
QUERY_BLOCK = 128


def solution(mesh):
    def local_block(x_blk, wqkv_blk, wout_blk, seg_blk):
        n_rows, local_cols = x_blk.shape
        local_heads = local_cols // HEAD_DIM
        n_blocks = n_rows // QUERY_BLOCK
        score_scale = 1.0 / HEAD_DIM ** 0.5
        x_rows = lax.all_gather(x_blk, "tp", axis=1, tiled=True)
        wqkv_cols = lax.all_gather(wqkv_blk, "sp", axis=0, tiled=True)
        qkv_proj = jnp.dot(x_rows, wqkv_cols, preferred_element_type=jnp.float32).astype(jnp.bfloat16)
        qkv_proj = qkv_proj.reshape(n_rows, local_heads, 3, HEAD_DIM)
        query_loc = qkv_proj[:, :, 0].reshape(n_blocks, QUERY_BLOCK, local_heads, HEAD_DIM)
        kv_all = lax.all_gather(qkv_proj[:, :, 1:], "sp", axis=0, tiled=True)
        seg_all = lax.all_gather(seg_blk, "sp", axis=0, tiled=True)
        key_all = kv_all[:, :, 0]
        value_all = kv_all[:, :, 1]
        positions = jnp.arange(kv_all.shape[0], dtype=jnp.int32)
        pos_query = (lax.axis_index("sp") * n_rows + jnp.arange(n_rows, dtype=jnp.int32)).reshape(n_blocks, QUERY_BLOCK)
        seg_query = seg_blk.reshape(n_blocks, QUERY_BLOCK)

        def one_block(block_args):
            query_blk, pos_blk, segq_blk = block_args
            scores = jnp.einsum("qnd,knd->nqk", query_blk, key_all, preferred_element_type=jnp.float32) * score_scale
            allowed = (positions[None, :] <= pos_blk[:, None]) & (seg_all[None, :] == segq_blk[:, None])
            scores = jnp.where(allowed[None], scores, -jnp.inf)
            prob_blk = jax.nn.softmax(scores, axis=-1).astype(jnp.bfloat16)
            return jnp.einsum("nqk,knd->qnd", prob_blk, value_all, preferred_element_type=jnp.float32).astype(jnp.bfloat16)

        context = lax.map(one_block, (query_loc, pos_query, seg_query)).reshape(n_rows, local_cols)
        context_rows = lax.all_gather(context, "tp", axis=1, tiled=True)
        wout_cols = lax.all_gather(wout_blk, "sp", axis=0, tiled=True)
        return jnp.dot(context_rows, wout_cols, preferred_element_type=jnp.float32).astype(jnp.bfloat16)

    row_spec = P(("dp", "sp"), "tp")
    return jax.shard_map(local_block, mesh=mesh, in_specs=(row_spec, P("sp", "tp"), P("sp", "tp"), P(("dp", "sp"))), out_specs=row_spec, check_vma=False)
```

profile of v0, /device:TPU:7, one launch (start us, length us, event | category | flops | bytes accessed | tf_op | source)
XLA Modules:
  0.0 866.6 jit_solution(11235561245325337369)
XLA Ops:
  6.5 0.7 all-gather.6.cloned.1.call-update
  7.3 0.7 all-gather.8.cloned.1.call-update
  8.1 151.7 %all-gather.6.cloned.1.call-done = bf16[1024,4096]{1,0:T(8,128)(2,1)} async-done(((bf16[1024,1024]{1,0:T(8,128)(2,1)}), bf16[1024,4096]{1,0:T(8,128)(2,1)}) %all-gather.6.cloned.1.call-update) | async-done | bytes 8388624 | tf_op jit(solution)/shard_map/all_gather | solution.py:16
  159.7 155.0 %all-gather.8.cloned.1.call-done = bf16[4096,3072]{1,0:T(8,128)(2,1)} async-done(((bf16[1024,3072]{1,0:T(8,128)(2,1)}), bf16[4096,3072]{1,0:T(8,128)(2,1)}) %all-gather.8.cloned.1.call-update) | async-done | bytes 25165840 | tf_op jit(solution)/shard_map/all_gather | solution.py:17
  314.8 33.1 %convolution_convert_fusion = bf16[1024,3072]{1,0:T(8,128)(2,1)} fusion(bf16[1024,4096]{1,0:T(8,128)(2,1)} %all-gather.6.cloned.1.call-done, bf16[4096,3072]{1,0:T(8,128)(2,1)} %all-gather.8.cloned.1.call-done), kind=kOutput, calls=%fused_computation.27 | convolution fusion | flops 25772949504 | bytes 39845888 | tf_op jit(solution)/shard_map/dot_general | solution.py:18
  347.8 8.6 copy.12
  356.5 4.9 slice.17
  361.4 0.5 all-gather.14.cloned.1.call-update
  362.0 5.4 all_gather.18
  367.4 1.9 slice.16
  369.3 3.0 copy.13
  372.3 96.1 %all-gather.10.cloned.1.call-done = bf16[4096,8,2,128]{0,3,2,1:T(8,128)(2,1)} async-done(((bf16[1024,8,2,128]{0,3,2,1:T(8,128)(2,1)}), bf16[4096,8,2,128]{0,3,2,1:T(8,128)(2,1)}) %all-gather.10.cloned.1.call-update) | async-done | bytes 16777232 | tf_op jit(solution)/shard_map/all_gather | solution.py:21
  468.5 11.7 %slice_bitcast_fusion = (bf16[4096,8,128]{0,2,1:T(8,128)(2,1)}, bf16[4096,8,128]{0,2,1:T(8,128)(2,1)}) fusion(bf16[4096,8,2,128]{0,3,2,1:T(8,128)(2,1)} %all-gather.10.cloned.1.call-done), kind=kLoop, calls=%fused_computation.25 | loop fusion | bytes 33554432 | tf_op jit(solution)/shard_map/squeeze | solution.py:24
  480.2 12.0 %copy.15 = bf16[4096,8,128]{2,0,1:T(8,128)(2,1)} copy(bf16[4096,8,128]{0,2,1:T(8,128)(2,1)} %get-tuple-element.108) | data formatting | bytes 16777216
  492.2 12.1 %copy.16 = bf16[4096,8,128]{2,0,1:T(8,128)(2,1)} copy(bf16[4096,8,128]{0,2,1:T(8,128)(2,1)} %get-tuple-element.107) | data formatting | bytes 16777216
  504.3 188.9 %while.11 = (s32[]{:T(128)}, bf16[8,128,8,128]{3,2,1,0:T(8,128)(2,1)S(1)}, s32[8,128]{1,0:T(8,128)S(1)}, s32[4096]{0:T(1024)S(1)}, s32[8,128]{1,0:T(8,128)S(1)},...) while((s32[]{:T(128)}, ...), condition=%wide.region_3.4_spmd.clone, body=%wide.region_0.3_spmd.clone.sunk | while | flops 2174357504 | bytes 52980840 | solution.py:37
  504.3 0.5 fusion.35
  504.8 1.0 constant_dynamic-slice_fusion.4
  505.8 11.4 %fusion.36 = (f32[8,128]{1,0:T(8,128)S(1)}, f32[8,128,4096]{2,1,0:T(8,128)}) fusion(pred[128,4096]{1,0:T(8,128)(4,1)S(1)} %fusion.35, bf16[4096,8,128]{2,0,1:T(8,128)(2,1)} %get-tuple-element.190, bf16[1,128,8,128]{3,2,1,0:T(8,128)(2,1)S(1)} %constant_dynamic-slice_fusion.4), kind=kOutput, calls=%fused_computation.31.clone.1 | convolution fusion | flops 1090523136 | bytes 25956352 | tf_op jit(solution)/shard_map/while/body/eval_jaxpr/sub | solution.py:34
  517.1 10.6 %fusion.37 = bf16[1,128,8,128]{3,1,2,0:T(8,128)(2,1)S(1)} fusion(bf16[4096,8,128]{2,0,1:T(8,128)(2,1)} %get-tuple-element.191, f32[8,128,4096]{2,1,0:T(8,128)} %get-tuple-element.164, f32[8,128]{1,0:T(8,128)S(1)} %get-tuple-element.165), kind=kOutput, calls=%fused_computation.13.clone.1 | convolution fusion | flops 1082261504 | bytes 25432064 | tf_op jit(solution)/shard_map/while/body/eval_jaxpr/nqk,knd->qnd/dot_general | solution.py:35
  527.9 0.5 fusion.35
  528.4 1.0 constant_dynamic-slice_fusion.4
  529.4 11.4 %fusion.36 = (f32[8,128]{1,0:T(8,128)S(1)}, f32[8,128,4096]{2,1,0:T(8,128)}) fusion(pred[128,4096]{1,0:T(8,128)(4,1)S(1)} %fusion.35, bf16[4096,8,128]{2,0,1:T(8,128)(2,1)} %get-tuple-element.190, bf16[1,128,8,128]{3,2,1,0:T(8,128)(2,1)S(1)} %constant_dynamic-slice_fusion.4), kind=kOutput, calls=%fused_computation.31.clone.1 | convolution fusion | flops 1090523136 | bytes 25956352 | tf_op jit(solution)/shard_map/while/body/eval_jaxpr/sub | solution.py:34
  540.7 10.6 %fusion.37 = bf16[1,128,8,128]{3,1,2,0:T(8,128)(2,1)S(1)} fusion(bf16[4096,8,128]{2,0,1:T(8,128)(2,1)} %get-tuple-element.191, f32[8,128,4096]{2,1,0:T(8,128)} %get-tuple-element.164, f32[8,128]{1,0:T(8,128)S(1)} %get-tuple-element.165), kind=kOutput, calls=%fused_computation.13.clone.1 | convolution fusion | flops 1082261504 | bytes 25432064 | tf_op jit(solution)/shard_map/while/body/eval_jaxpr/nqk,knd->qnd/dot_general | solution.py:35
  551.5 0.5 fusion.35
  552.0 1.0 constant_dynamic-slice_fusion.4
  553.0 11.4 %fusion.36 = (f32[8,128]{1,0:T(8,128)S(1)}, f32[8,128,4096]{2,1,0:T(8,128)}) fusion(pred[128,4096]{1,0:T(8,128)(4,1)S(1)} %fusion.35, bf16[4096,8,128]{2,0,1:T(8,128)(2,1)} %get-tuple-element.190, bf16[1,128,8,128]{3,2,1,0:T(8,128)(2,1)S(1)} %constant_dynamic-slice_fusion.4), kind=kOutput, calls=%fused_computation.31.clone.1 | convolution fusion | flops 1090523136 | bytes 25956352 | tf_op jit(solution)/shard_map/while/body/eval_jaxpr/sub | solution.py:34
  564.4 10.6 %fusion.37 = bf16[1,128,8,128]{3,1,2,0:T(8,128)(2,1)S(1)} fusion(bf16[4096,8,128]{2,0,1:T(8,128)(2,1)} %get-tuple-element.191, f32[8,128,4096]{2,1,0:T(8,128)} %get-tuple-element.164, f32[8,128]{1,0:T(8,128)S(1)} %get-tuple-element.165), kind=kOutput, calls=%fused_computation.13.clone.1 | convolution fusion | flops 1082261504 | bytes 25432064 | tf_op jit(solution)/shard_map/while/body/eval_jaxpr/nqk,knd->qnd/dot_general | solution.py:35
  575.7 1.0 constant_dynamic-slice_fusion.4
  576.6 11.4 %fusion.36 = (f32[8,128]{1,0:T(8,128)S(1)}, f32[8,128,4096]{2,1,0:T(8,128)}) fusion(pred[128,4096]{1,0:T(8,128)(4,1)S(1)} %fusion.35, bf16[4096,8,128]{2,0,1:T(8,128)(2,1)} %get-tuple-element.190, bf16[1,128,8,128]{3,2,1,0:T(8,128)(2,1)S(1)} %constant_dynamic-slice_fusion.4), kind=kOutput, calls=%fused_computation.31.clone.1 | convolution fusion | flops 1090523136 | bytes 25956352 | tf_op jit(solution)/shard_map/while/body/eval_jaxpr/sub | solution.py:34
  588.0 10.6 %fusion.37 = bf16[1,128,8,128]{3,1,2,0:T(8,128)(2,1)S(1)} fusion(bf16[4096,8,128]{2,0,1:T(8,128)(2,1)} %get-tuple-element.191, f32[8,128,4096]{2,1,0:T(8,128)} %get-tuple-element.164, f32[8,128]{1,0:T(8,128)S(1)} %get-tuple-element.165), kind=kOutput, calls=%fused_computation.13.clone.1 | convolution fusion | flops 1082261504 | bytes 25432064 | tf_op jit(solution)/shard_map/while/body/eval_jaxpr/nqk,knd->qnd/dot_general | solution.py:35
  599.3 1.0 constant_dynamic-slice_fusion.4
  600.3 11.4 %fusion.36 = (f32[8,128]{1,0:T(8,128)S(1)}, f32[8,128,4096]{2,1,0:T(8,128)}) fusion(pred[128,4096]{1,0:T(8,128)(4,1)S(1)} %fusion.35, bf16[4096,8,128]{2,0,1:T(8,128)(2,1)} %get-tuple-element.190, bf16[1,128,8,128]{3,2,1,0:T(8,128)(2,1)S(1)} %constant_dynamic-slice_fusion.4), kind=kOutput, calls=%fused_computation.31.clone.1 | convolution fusion | flops 1090523136 | bytes 25956352 | tf_op jit(solution)/shard_map/while/body/eval_jaxpr/sub | solution.py:34
  611.6 10.6 %fusion.37 = bf16[1,128,8,128]{3,1,2,0:T(8,128)(2,1)S(1)} fusion(bf16[4096,8,128]{2,0,1:T(8,128)(2,1)} %get-tuple-element.191, f32[8,128,4096]{2,1,0:T(8,128)} %get-tuple-element.164, f32[8,128]{1,0:T(8,128)S(1)} %get-tuple-element.165), kind=kOutput, calls=%fused_computation.13.clone.1 | convolution fusion | flops 1082261504 | bytes 25432064 | tf_op jit(solution)/shard_map/while/body/eval_jaxpr/nqk,knd->qnd/dot_general | solution.py:35
  622.4 0.5 fusion.35
  622.9 1.0 constant_dynamic-slice_fusion.4
  623.9 11.4 %fusion.36 = (f32[8,128]{1,0:T(8,128)S(1)}, f32[8,128,4096]{2,1,0:T(8,128)}) fusion(pred[128,4096]{1,0:T(8,128)(4,1)S(1)} %fusion.35, bf16[4096,8,128]{2,0,1:T(8,128)(2,1)} %get-tuple-element.190, bf16[1,128,8,128]{3,2,1,0:T(8,128)(2,1)S(1)} %constant_dynamic-slice_fusion.4), kind=kOutput, calls=%fused_computation.31.clone.1 | convolution fusion | flops 1090523136 | bytes 25956352 | tf_op jit(solution)/shard_map/while/body/eval_jaxpr/sub | solution.py:34
  635.2 10.6 %fusion.37 = bf16[1,128,8,128]{3,1,2,0:T(8,128)(2,1)S(1)} fusion(bf16[4096,8,128]{2,0,1:T(8,128)(2,1)} %get-tuple-element.191, f32[8,128,4096]{2,1,0:T(8,128)} %get-tuple-element.164, f32[8,128]{1,0:T(8,128)S(1)} %get-tuple-element.165), kind=kOutput, calls=%fused_computation.13.clone.1 | convolution fusion | flops 1082261504 | bytes 25432064 | tf_op jit(solution)/shard_map/while/body/eval_jaxpr/nqk,knd->qnd/dot_general | solution.py:35
  646.5 1.0 constant_dynamic-slice_fusion.4
  647.5 11.4 %fusion.36 = (f32[8,128]{1,0:T(8,128)S(1)}, f32[8,128,4096]{2,1,0:T(8,128)}) fusion(pred[128,4096]{1,0:T(8,128)(4,1)S(1)} %fusion.35, bf16[4096,8,128]{2,0,1:T(8,128)(2,1)} %get-tuple-element.190, bf16[1,128,8,128]{3,2,1,0:T(8,128)(2,1)S(1)} %constant_dynamic-slice_fusion.4), kind=kOutput, calls=%fused_computation.31.clone.1 | convolution fusion | flops 1090523136 | bytes 25956352 | tf_op jit(solution)/shard_map/while/body/eval_jaxpr/sub | solution.py:34
  658.9 10.6 %fusion.37 = bf16[1,128,8,128]{3,1,2,0:T(8,128)(2,1)S(1)} fusion(bf16[4096,8,128]{2,0,1:T(8,128)(2,1)} %get-tuple-element.191, f32[8,128,4096]{2,1,0:T(8,128)} %get-tuple-element.164, f32[8,128]{1,0:T(8,128)S(1)} %get-tuple-element.165), kind=kOutput, calls=%fused_computation.13.clone.1 | convolution fusion | flops 1082261504 | bytes 25432064 | tf_op jit(solution)/shard_map/while/body/eval_jaxpr/nqk,knd->qnd/dot_general | solution.py:35
  669.6 0.5 fusion.35
  670.1 1.0 constant_dynamic-slice_fusion.4
  671.1 11.4 %fusion.36 = (f32[8,128]{1,0:T(8,128)S(1)}, f32[8,128,4096]{2,1,0:T(8,128)}) fusion(pred[128,4096]{1,0:T(8,128)(4,1)S(1)} %fusion.35, bf16[4096,8,128]{2,0,1:T(8,128)(2,1)} %get-tuple-element.190, bf16[1,128,8,128]{3,2,1,0:T(8,128)(2,1)S(1)} %constant_dynamic-slice_fusion.4), kind=kOutput, calls=%fused_computation.31.clone.1 | convolution fusion | flops 1090523136 | bytes 25956352 | tf_op jit(solution)/shard_map/while/body/eval_jaxpr/sub | solution.py:34
  682.5 10.6 %fusion.37 = bf16[1,128,8,128]{3,1,2,0:T(8,128)(2,1)S(1)} fusion(bf16[4096,8,128]{2,0,1:T(8,128)(2,1)} %get-tuple-element.191, f32[8,128,4096]{2,1,0:T(8,128)} %get-tuple-element.164, f32[8,128]{1,0:T(8,128)S(1)} %get-tuple-element.165), kind=kOutput, calls=%fused_computation.13.clone.1 | convolution fusion | flops 1082261504 | bytes 25432064 | tf_op jit(solution)/shard_map/while/body/eval_jaxpr/nqk,knd->qnd/dot_general | solution.py:35
  693.2 1.9 copy.35
  695.2 150.3 %all-gather.12.cloned.1.call-done = bf16[1024,4096]{1,0:T(8,128)(2,1)} async-done(((bf16[1024,1024]{1,0:T(8,128)(2,1)}), bf16[1024,4096]{1,0:T(8,128)(2,1)}) %all-gather.12.cloned.1.call-update) | async-done | bytes 8388624 | tf_op jit(solution)/shard_map/all_gather | solution.py:38
  845.5 14.6 %convolution_convert_fusion.1 = bf16[1024,1024]{1,0:T(8,128)(2,1)} fusion(bf16[1024,4096]{1,0:T(8,128)(2,1)} %all-gather.12.cloned.1.call-done, bf16[4096,1024]{1,0:T(8,128)(2,1)} %all-gather.14.cloned.1.call-done), kind=kOutput, calls=%fused_computation.29 | convolution fusion | flops 8590983168 | bytes 18874368 | tf_op jit(solution)/shard_map/dot_general | solution.py:40
  (33 shorter events, 3.3 us)
Async XLA Ops:
  6.5 153.2 %all-gather.6.cloned.1.call-start = ((), (), s32[]{:S(2)}) async-start(), calls=%async_computation | async-start | bytes 10485760 | tf_op jit(solution)/shard_map/all_gather | solution.py:16
  7.3 307.5 %all-gather.8.cloned.1.call-start = ((), (), s32[]{:S(2)}) async-start(), calls=%async_computation.1 | async-start | bytes 31457280 | tf_op jit(solution)/shard_map/all_gather | solution.py:17
  8.0 460.5 %all-gather.10.cloned.1.call-start = ((), (), s32[]{:S(2)}) async-start(), calls=%async_computation.2 | async-start | bytes 20971520 | tf_op jit(solution)/shard_map/all_gather | solution.py:21
  356.5 5.5 copy-start.1
  361.3 333.9 %all-gather.14.cloned.1.call-start = ((), (), s32[]{:S(2)}) async-start(), calls=%async_computation.4 | async-start | bytes 10485760 | tf_op jit(solution)/shard_map/all_gather | solution.py:39
  361.9 483.6 %all-gather.12.cloned.1.call-start = ((), (), s32[]{:S(2)}) async-start(), calls=%async_computation.3 | async-start | bytes 10485760 | tf_op jit(solution)/shard_map/all_gather | solution.py:38
  492.2 12.1 %copy-start = (bf16[8,128,8,128]{3,2,1,0:T(8,128)(2,1)S(1)}, bf16[8,128,8,128]{3,2,1,0:T(8,128)(2,1)}, u32[]{:S(2)}) copy-start(bf16[8,128,8,128]{3,2,1,0:T(8,128)(2,1)} %custom-call) | copy-start | bytes 6291460
Sparse Core Ops, SparseCore 0:
  8.9 150.7 all-gather.5
  161.3 153.4 all-gather.7
  361.5 106.9 all-gather.9
  469.9 58.4 all-gather.13
  695.3 150.1 all-gather.11
where the time goes:
time: 869 us; the launch traced here: 867 us
  waiting for transfers between devices  555 us (64%)
  matrix products  223 us (26%)
  local copies, waits for them, and re-layouts  65.5 us (8%)
  between operations  13.2 us (2%)
    all_gather x1, waiting for transfers between devices, local_block(): wqkv_cols = lax.all_gather(wqkv_blk, 'sp', axis=0, tiled=True)  155 us
    all_gather x1, waiting for transfers between devices, local_block(): x_rows = lax.all_gather(x_blk, 'tp', axis=1, tiled=True)  152 us
    all_gather x1, waiting for transfers between devices, local_block(): context_rows = lax.all_gather(context, 'tp', axis=1, tiled=True)  150 us
    all_gather x1, waiting for transfers between devices, local_block(): kv_all = lax.all_gather(qkv_proj[:, :, 1:], 'sp', axis=0, tiled=True)  96.1 us
    sub x8, matrix products, one_block(): prob_blk = jax.nn.softmax(scores, axis=-1).astype(jnp.bfloat16)  90.9 us
    dot_general x8, matrix products, one_block(): jnp.einsum('nqk,knd->qnd', prob_blk, value_all, preferred_element_type=jn...  84.5 us
    dot_general x1, matrix products, local_block(): jnp.dot(x_rows, wqkv_cols, preferred_element_type=jnp.float32)  33.1 us
    unnamed x7, local copies, waits for them, and re-layouts  26 us
  transfers between devices with their start and end apart: 5, of which 4 were waited for; matrix products, arithmetic and copies ran while one was open for 27% of the time, Pallas kernels for 0%

commit v1 on v0

v1 whole, which is shorter than its diff:
```python
import functools

import jax
import jax.numpy as jnp
from jax import lax
from jax.experimental import pallas as pl
from jax.experimental.pallas import tpu as pltpu
from jax.sharding import PartitionSpec as P

HEAD_DIM = 128
NT = 4
NR = 8
NP = 4
LOG2E = 1.4426950408889634
MIB = 1024 * 1024


def _mo(i, n):
    return pl.multiple_of(i * n, n)


def _gather_dot(qkv, x_hbm, w_hbm, seg_hbm, *refs):
    if qkv:
        q_ref, kv_all, seg_all = refs[:3]
        refs = refs[3:]
    else:
        (y_ref,) = refs[:1]
        refs = refs[1:]
    xg, wg = refs[:2]
    refs = refs[2:]
    if qkv:
        kv = refs[0]
        refs = refs[1:]
    loc, xs, xl, xr, ws_own, ws_y, ws_x, ws_f, wr_own, wr_y, wr_x, wr_f = refs[:12]
    if qkv:
        kv_send, kv_yr, kv_cr, kv_fs, kv_fr, seg_s, seg_r = refs[12:]

    R, C = x_hbm.shape
    N = w_hbm.shape[1]
    RC, NG, NH = R // NR, N // NP, N // (2 * NP)
    d, t, s = lax.axis_index("dp"), lax.axis_index("tp"), lax.axis_index("sp")
    yc, c = s // 2, s % 2
    sib, ynb, diag = s + 1 - 2 * c, s + 2 - 4 * yc, (2 - 2 * yc) + (1 - c)
    mesh_id = pl.DeviceIdType.MESH
    to_sib, to_y, to_diag = (d, t, sib), (d, t, ynb), (d, t, diag)
    to_x = (1 - d, t, s)
    to_right, to_left = (d, t + 1, s), (d, t - 1, s)
    has_right, has_left = t < NT - 1, t > 0

    bar = pltpu.get_barrier_semaphore()

    def greet(who):
        pl.semaphore_signal(bar, inc=1, device_id=who, device_id_type=mesh_id)

    greet(to_sib)
    greet(to_y)
    greet(to_x)
    if qkv:
        greet(to_diag)

    @pl.when(has_right)
    def _():
        greet(to_right)

    @pl.when(has_left)
    def _():
        greet(to_left)

    base = 4 if qkv else 3

    @pl.when(has_right & has_left)
    def _():
        pl.semaphore_wait(bar, base + 2)

    @pl.when(jnp.logical_not(has_right & has_left))
    def _():
        pl.semaphore_wait(bar, base + 1)

    def remote(src, dst, send, recv, who):
        return pltpu.make_async_remote_copy(src, dst, send, recv, device_id=who, device_id_type=mesh_id)

    def w_own(p):
        cols = pl.ds(p * NG, NG)
        return remote(w_hbm.at[:, cols], wg.at[s, :, cols], ws_own.at[p], wr_own.at[p], to_sib)

    def w_own_in(p):
        cols = pl.ds(p * NG, NG)
        return remote(w_hbm.at[:, cols], wg.at[sib, :, cols], ws_own.at[p], wr_own.at[p], to_sib)

    def mine(p):
        return pl.ds(_mo(2 * p + d, NH), NH)

    def other(p):
        return pl.ds(_mo(2 * p + 1 - d, NH), NH)

    def w_y(p):
        return remote(w_hbm.at[:, mine(p)], wg.at[s, :, mine(p)], ws_y.at[p], wr_y.at[p], to_y)

    def w_y_in(p):
        return remote(w_hbm.at[:, mine(p)], wg.at[ynb, :, mine(p)], ws_y.at[p], wr_y.at[p], to_y)

    def w_x(p):
        return remote(wg.at[ynb, :, mine(p)], wg.at[ynb, :, mine(p)], ws_x.at[p], wr_x.at[p], to_x)

    def w_x_in(p):
        return remote(wg.at[ynb, :, other(p)], wg.at[ynb, :, other(p)], ws_x.at[p], wr_x.at[p], to_x)

    def w_f(p, which):
        cols = mine(p) if which == 0 else other(p)
        return remote(wg.at[ynb, :, cols], wg.at[ynb, :, cols], ws_f.at[which, p], wr_f.at[which, p], to_sib)

    def w_f_in(p, which):
        cols = mine(p) if which == 0 else other(p)
        return remote(wg.at[diag, :, cols], wg.at[diag, :, cols], ws_f.at[which, p], wr_f.at[which, p], to_sib)

    def rows(r):
        return pl.ds(_mo(r, RC), RC)

    def x_own(r, way):
        recv = xl if way == 0 else xr
        return remote(x_hbm.at[rows(r)], xg.at[t, rows(r)], xs.at[way, 0, r], recv.at[0, r], to_right if way == 0 else to_left)

    def x_arrive(r, way, dist):
        k = t - dist if way == 0 else t + dist
        recv = xl if way == 0 else xr
        return remote(xg.at[k, rows(r)], xg.at[k, rows(r)], xs.at[way, 0, r], recv.at[dist - 1, r], to_right if way == 0 else to_left)

    def x_forward(r, way, dist):
        k = t - dist if way == 0 else t + dist
        recv = xl if way == 0 else xr
        return remote(xg.at[k, rows(r)], xg.at[k, rows(r)], xs.at[way, dist, r], recv.at[dist, r], to_right if way == 0 else to_left)

    def send_own_x(r):
        @pl.when(has_right)
        def _():
            x_own(r, 0).start()

        @pl.when(has_left)
        def _():
            x_own(r, 1).start()

    def relay_x(r):
        for dist in range(1, NT):
            for way in range(2):
                here = (t >= dist) if way == 0 else (t <= NT - 1 - dist)

                @pl.when(here)
                def _():
                    x_arrive(r, way, dist).wait_recv()
                    if dist < NT - 1:
                        @pl.when(has_right if way == 0 else has_left)
                        def _():
                            x_forward(r, way, dist).start()

    own_x = pltpu.make_async_copy(x_hbm, xg.at[t], loc.at[0])
    own_w = pltpu.make_async_copy(w_hbm, wg.at[s], loc.at[1])
    for r in range(2):
        send_own_x(r)
    for p in range(NP):
        w_y(p).start()
    for p in range(NP):
        w_own(p).start()
    own_x.start()
    own_w.start()
    if qkv:
        own_seg = pltpu.make_async_copy(seg_hbm, seg_all.at[s], loc.at[3])
        own_seg.start()
        peers = ((to_sib, sib), (to_y, ynb), (to_diag, diag))

        def seg_out(i):
            return remote(seg_hbm, seg_all.at[s], seg_s.at[i], seg_r.at[i], peers[i][0])

        def seg_in(i):
            return remote(seg_hbm, seg_all.at[peers[i][1]], seg_s.at[i], seg_r.at[i], peers[i][0])

        for i in range(3):
            seg_out(i).start()

    def unit(r, p):
        cols = pl.ds(_mo(p, NG), NG)
        acc = jnp.dot(xg[0, rows(r), :], wg[0, :, cols], preferred_element_type=jnp.float32)
        for k in range(1, NT):
            acc += jnp.dot(xg[k, rows(r), :], wg[k, :, cols], preferred_element_type=jnp.float32)
        out = acc.astype(jnp.bfloat16)
        if qkv:
            for h in range(2):
                at = 3 * HEAD_DIM * h
                q_ref[rows(r), pl.ds(pl.multiple_of(p * (2 * HEAD_DIM) + h * HEAD_DIM, HEAD_DIM), HEAD_DIM)] = out[:, at : at + HEAD_DIM]
                kv[rows(r), pl.ds(_mo(2 * p + h, 2 * HEAD_DIM), 2 * HEAD_DIM)] = out[:, at + HEAD_DIM : at + 3 * HEAD_DIM]
        else:
            y_ref[rows(r), cols] = out

    def kv_cols(p):
        return pl.ds(_mo(p, 4 * HEAD_DIM), 4 * HEAD_DIM)

    def kv_unit(r, p, who, send, recv):
        return remote(kv.at[rows(r), kv_cols(p)], kv_all.at[s, rows(r), kv_cols(p)], send, recv, who)

    def send_unit(r, p):
        pltpu.make_async_copy(kv.at[rows(r), kv_cols(p)], kv_all.at[s, rows(r), kv_cols(p)], loc.at[2]).start()

        @pl.when(yc == 0)
        def _():
            kv_unit(r, p, to_y, kv_send.at[0], kv_yr.at[r]).start()

        @pl.when(c == 0)
        def _():
            kv_unit(r, p, to_sib, kv_send.at[1], kv_cr.at[r]).start()

    def do_units(work):
        for n, f in work:
            def body(u, z, f=f):
                unit(*f(u))
                return z
            lax.fori_loop(0, n, body, 0)
        if qkv:
            for n, f in work:
                def body(u, z, f=f):
                    send_unit(*f(u))
                    return z
                lax.fori_loop(0, n, body, 0)

    def kv_row(r, owner, who, send, recv):
        return remote(kv_all.at[owner, rows(r)], kv_all.at[owner, rows(r)], send, recv, who)

    def pass_kv(r):
        if qkv:
            @pl.when(yc == 1)
            def _():
                kv_row(r, ynb, to_y, kv_fs.at[r], kv_yr.at[r]).wait_recv()
                kv_row(r, ynb, to_sib, kv_fs.at[r], kv_fr.at[r]).start()

    def relay_w(i):
        if i < NP:
            w_y_in(i).wait_recv()
            w_x(i).start()
            w_f(i, 0).start()
        if 1 <= i <= NP:
            w_x_in(i - 1).wait_recv()
            w_f(i - 1, 1).start()
            p = i - 1
            if p == 0:
                own_x.wait()
                own_w.wait()
            w_own_in(p).wait_recv()
            w_f_in(p, 0).wait_recv()
            w_f_in(p, 1).wait_recv()

    for i in range(NP + 1):
        relay_x(i)
        send_own_x(i + 2)
        relay_w(i)
        if i == 2:
            do_units([(6, lambda u: (u // 2, u % 2))])
        if i == 3:
            do_units([(2, lambda u: (3, u)), (4, lambda u: (u, 2))])
        if i == 4:
            do_units([(3, lambda u: (4, u)), (5, lambda u: (u, 3))])

    def late(i, z):
        relay_x(i)

        @pl.when(i + 2 < NR)
        def _():
            send_own_x(i + 2)

        pass_kv(2 * (i - NP - 1))
        pass_kv(2 * (i - NP - 1) + 1)
        do_units([(NP, lambda u: (i, u))])
        return z

    lax.fori_loop(NP + 1, NR, late, 0)

    for p in range(NP):
        w_own(p).wait_send()
        w_y(p).wait_send()
        w_x(p).wait_send()
        w_f(p, 0).wait_send()
        w_f(p, 1).wait_send()

    def drain_x(r, z):
        @pl.when(has_right)
        def _():
            x_own(r, 0).wait_send()
            for dist in range(1, NT - 1):
                @pl.when(t >= dist)
                def _():
                    x_forward(r, 0, dist).wait_send()

        @pl.when(has_left)
        def _():
            x_own(r, 1).wait_send()
            for dist in range(1, NT - 1):
                @pl.when(t <= NT - 1 - dist)
                def _():
                    x_forward(r, 1, dist).wait_send()

        return z

    lax.fori_loop(0, NR, drain_x, 0)
    if qkv:
        pass_kv(6)
        pass_kv(7)
        own_seg.wait()
        for i in range(3):
            seg_out(i).wait_send()
            seg_in(i).wait_recv()
        pltpu.make_async_copy(kv, kv_all.at[s], loc.at[2]).wait()

        @pl.when(yc == 0)
        def _():
            remote(kv, kv_all.at[s], kv_send.at[0], kv_yr.at[0], to_y).wait_send()

        @pl.when(c == 0)
        def _():
            remote(kv, kv_all.at[s], kv_send.at[1], kv_cr.at[0], to_sib).wait_send()

        def drain_kv(r, z):
            @pl.when(c == 1)
            def _():
                kv_row(r, sib, to_sib, kv_fs.at[r], kv_cr.at[r]).wait_recv()

            @pl.when(yc == 1)
            def _():
                kv_row(r, ynb, to_sib, kv_fs.at[r], kv_fr.at[r]).wait_send()
                kv_row(r, diag, to_sib, kv_fs.at[r], kv_fr.at[r]).wait_recv()

            return z

        lax.fori_loop(0, NR, drain_kv, 0)


def _gather_call(qkv, x, w, seg):
    R, C = x.shape
    N = w.shape[1]
    dma = pltpu.SemaphoreType.DMA
    hbm = pl.BlockSpec(memory_space=pltpu.HBM)
    vmem = pl.BlockSpec(memory_space=pltpu.VMEM)
    bf16 = jnp.bfloat16
    scratch = [pltpu.VMEM((NT, R, C), bf16), pltpu.VMEM((NT, C, N), bf16)]
    if qkv:
        heads = N // (3 * HEAD_DIM)
        out_shape = (
            jax.ShapeDtypeStruct((R, heads * HEAD_DIM), bf16),
            jax.ShapeDtypeStruct((NT, R, 2 * heads * HEAD_DIM), bf16),
            jax.ShapeDtypeStruct((NT,) + seg.shape, jnp.int32),
        )
        out_specs = (vmem, hbm, hbm)
        scratch.append(pltpu.VMEM((R, 2 * heads * HEAD_DIM), bf16))
    else:
        out_shape = jax.ShapeDtypeStruct((R, N), bf16)
        out_specs = vmem
    scratch += [dma((4,)), dma((2, 3, NR)), dma((3, NR)), dma((3, NR)), dma((NP,)), dma((NP,)), dma((NP,)), dma((2, NP)),
                dma((NP,)), dma((NP,)), dma((NP,)), dma((2, NP))]
    if qkv:
        scratch += [dma((2,)), dma((NR,)), dma((NR,)), dma((NR,)), dma((NR,)), dma((3,)), dma((3,))]
    return pl.pallas_call(
        functools.partial(_gather_dot, qkv),
        out_shape=out_shape,
        in_specs=[hbm, hbm, hbm],
        out_specs=out_specs,
        scratch_shapes=scratch,
        compiler_params=pltpu.CompilerParams(collective_id=0 if qkv else 1, has_side_effects=True, vmem_limit_bytes=60 * MIB),
        cost_estimate=pl.CostEstimate(flops=2 * R * NT * C * N, bytes_accessed=2 * NT * (R * C + C * N), transcendentals=0),
        name="qkv_dot" if qkv else "out_dot",
    )(x, w, seg)


def _attention(BQ, BK, s_ref, seg_ref, q_ref, kv_ref, o_ref, st_ref, sc_ref, m_ref, l_ref, acc_ref):
    R = q_ref.shape[0]
    s = s_ref[0]
    seg = seg_ref[...]
    scale = LOG2E / HEAD_DIM ** 0.5
    for doc in range(1, 4):
        st_ref[doc] = jnp.sum((seg < doc).astype(jnp.int32))

    def doc_start(row):
        out = jnp.zeros_like(row)
        for doc in range(1, 4):
            start = st_ref[doc]
            out = jnp.where(start <= row, jnp.maximum(out, start), out)
        return out

    def lane_groups(a, op):
        out = a[:, :HEAD_DIM]
        for g in range(1, a.shape[1] // HEAD_DIM):
            out = op(out, a[:, HEAD_DIM * g : HEAD_DIM * (g + 1)])
        return out

    def q_block(b, z):
        row0 = s * R + b * BQ
        q_at = pl.ds(_mo(b, BQ), BQ)
        lo = doc_start(row0) // BK
        hi = (row0 + BQ - 1) // BK + 1
        full_lo = jnp.clip((doc_start(row0 + BQ - 1) + BK - 1) // BK, lo, hi)
        full_hi = jnp.clip((row0 + 1) // BK, full_lo, hi)
        m_ref[...] = jnp.full(m_ref.shape, -3e38, jnp.float32)
        l_ref[...] = jnp.zeros(l_ref.shape, jnp.float32)
        acc_ref[...] = jnp.zeros(acc_ref.shape, jnp.float32)

        def scores(j, z, masked):
            k_at = pl.ds(_mo(j, BK), BK)
            if masked:
                row_id = row0 + lax.broadcasted_iota(jnp.int32, (BQ, 1), 0)
                key_id = j * BK + lax.broadcasted_iota(jnp.int32, (BQ, BK), 1)
                seen = (key_id <= row_id) & (key_id >= doc_start(row_id))
            for h in range(2):
                q = q_ref[q_at, HEAD_DIM * h : HEAD_DIM * (h + 1)]
                k = kv_ref[k_at, 2 * HEAD_DIM * h : 2 * HEAD_DIM * h + HEAD_DIM]
                sc = lax.dot_general(q, k, (((1,), (1,)), ((), ())), preferred_element_type=jnp.float32)
                if masked:
                    sc = jnp.where(seen, sc, -jnp.inf)
                sc_ref[h, j] = sc
                m_ref[h] = jnp.maximum(m_ref[h], lane_groups(sc, jnp.maximum))
            return z

        def weights(j, z):
            for h in range(2):
                m = m_ref[h]
                e = jnp.exp2((sc_ref[h, j] - jnp.concatenate([m] * (BK // HEAD_DIM), axis=1)) * scale)
                sc_ref[h, j] = e
                l_ref[h] = l_ref[h] + lane_groups(e, jnp.add)
            return z

        def values(j, z):
            k_at = pl.ds(_mo(j, BK), BK)
            for h in range(2):
                v = kv_ref[k_at, 2 * HEAD_DIM * h + HEAD_DIM : 2 * HEAD_DIM * (h + 1)]
                p = (sc_ref[h, j] * jnp.concatenate([l_ref[h]] * (BK // HEAD_DIM), axis=1)).astype(jnp.bfloat16)
                acc_ref[h] = acc_ref[h] + jnp.dot(p, v, preferred_element_type=jnp.float32)
            return z

        lax.fori_loop(lo, full_lo, functools.partial(scores, masked=True), 0)
        lax.fori_loop(full_lo, full_hi, functools.partial(scores, masked=False), 0)
        lax.fori_loop(full_hi, hi, functools.partial(scores, masked=True), 0)
        for h in range(2):
            m_ref[h] = jnp.broadcast_to(jnp.max(m_ref[h], axis=1, keepdims=True), (BQ, HEAD_DIM))
        lax.fori_loop(lo, hi, weights, 0)
        for h in range(2):
            l_ref[h] = jnp.broadcast_to(1.0 / jnp.sum(l_ref[h], axis=1, keepdims=True), (BQ, HEAD_DIM))
        lax.fori_loop(lo, hi, values, 0)
        for h in range(2):
            o_ref[q_at, HEAD_DIM * h : HEAD_DIM * (h + 1)] = acc_ref[h].astype(jnp.bfloat16)
        return z

    lax.fori_loop(0, R // BQ, q_block, 0)


def _attention_call(q, kv_all, seg_all):
    R, cols = q.shape
    rows = NT * R
    BQ, BK = min(512, R), min(512, R)
    s = lax.axis_index("sp").astype(jnp.int32).reshape(1)
    return pl.pallas_call(
        functools.partial(_attention, BQ, BK),
        out_shape=jax.ShapeDtypeStruct((R, cols), jnp.bfloat16),
        grid_spec=pltpu.PrefetchScalarGridSpec(
            num_scalar_prefetch=1,
            grid=(cols // (2 * HEAD_DIM),),
            in_specs=[
                pl.BlockSpec(seg_all.shape, lambda p, s: (0, 0)),
                pl.BlockSpec((R, 2 * HEAD_DIM), lambda p, s: (0, p)),
                pl.BlockSpec((rows, 4 * HEAD_DIM), lambda p, s: (0, p)),
            ],
            out_specs=pl.BlockSpec((R, 2 * HEAD_DIM), lambda p, s: (0, p)),
            scratch_shapes=[
                pltpu.SMEM((4,), jnp.int32),
                pltpu.VMEM((2, rows // BK, BQ, BK), jnp.float32),
                pltpu.VMEM((2, BQ, HEAD_DIM), jnp.float32),
                pltpu.VMEM((2, BQ, HEAD_DIM), jnp.float32),
                pltpu.VMEM((2, BQ, HEAD_DIM), jnp.float32),
            ],
        ),
        compiler_params=pltpu.CompilerParams(vmem_limit_bytes=48 * MIB),
        cost_estimate=pl.CostEstimate(flops=2 * R * rows * cols, bytes_accessed=4 * rows * cols, transcendentals=R * rows * cols // 256),
        name="attention",
    )(s, seg_all, q, kv_all)


def solution(mesh):
    def local_block(x_blk, wqkv_blk, wout_blk, seg_blk):
        R = x_blk.shape[0]
        seg = seg_blk.reshape(-1, 128)
        q, kv_all, seg_all = _gather_call(True, x_blk, wqkv_blk, seg)
        context = _attention_call(q, kv_all.reshape(NT * R, -1), seg_all.reshape(-1, 128))
        return _gather_call(False, context, wout_blk, seg)

    row_spec = P(("dp", "sp"), "tp")
    return jax.shard_map(local_block, mesh=mesh, in_specs=(row_spec, P("sp", "tp"), P("sp", "tp"), P(("dp", "sp"))), out_specs=row_spec, check_vma=False)
```

time: 869 us -> 376 us (0.43)
  the two profiles are of different devices: /device:TPU:7 before, /device:TPU:4 now
where the time goes in v1:
time: 376 us; the launch traced here: 371 us
  Pallas kernels  364 us (97%)
  local copies, waits for them, and re-layouts  6.7 us (2%)
    pallas_call x2, Pallas kernels, _gather_call(): pl.pallas_call(functools.partial(_gather_dot, qkv), out_shape=out_shape,...  330 us
    pallas_call x1, Pallas kernels, _attention_call(): pl.pallas_call(functools.partial(_attention, BQ, BK), out_shape=jax.Shape...  33.9 us

profile of v1, /device:TPU:4, one launch (start us, length us, event | category | flops | bytes accessed | tf_op | source)
XLA Modules:
  0.0 370.6 jit_solution(14975212905014143818)
XLA Ops:
  0.0 171.0 %qkv_dot.1 = (bf16[1024,1024]{1,0:T(8,128)(2,1)}, bf16[4,1024,2048]{2,1,0:T(8,128)(2,1)}, s32[4,8,128]{2,1,0:T(8,128)}) custom-call(bf16[1024,1024]{1,0:T(8,128)(2,1)} %x_hbm.1, bf16[1024,3072]{1,0:T(8,128)(2,1)} %w_hbm.2, s32[8,128]{1,0:T(8,128)} %bitcast.5), custom_call_target="tpu_custom_call" | custom-call | flops 25769803776 | bytes 33554432 | tf_op jit(solution)/shard_map/qkv_dot/pallas_call | solution.py:357
  171.0 0.0 copy-start
  171.0 0.7 copy-done
  171.7 0.0 copy-start.1
  171.7 1.6 copy-done.1
  173.3 33.9 %attention.1.x_hbm = bf16[1024,1024]{1,0:T(8,128)(2,1)S(1)} custom-call(s32[1]{0:T(128)} %bitcast.s_ref, s32[32,128]{1,0:T(8,128)S(1)} %bitcast.4, bf16[1024,1024]{1,0:T(8,128)(2,1)S(1)} %copy-done.1, bf16[4096,2048]{1,0:T(8,128)(2,1)} %bitcast.7), custom_call_target="tpu_custom_call" | custom-call | flops 8589934592 | bytes 16777216 | tf_op jit(solution)/shard_map/attention/pallas_call | solution.py:454
  207.1 0.0 copy-start.2
  207.2 1.3 copy-done.2
  208.5 159.0 %out_dot.1 = bf16[1024,1024]{1,0:T(8,128)(2,1)} custom-call(bf16[1024,1024]{1,0:T(8,128)(2,1)} %copy-done.2, bf16[1024,1024]{1,0:T(8,128)(2,1)} %w_hbm.3, s32[8,128]{1,0:T(8,128)} %bitcast.6), custom_call_target="tpu_custom_call" | custom-call | flops 8589934592 | bytes 16777216 | tf_op jit(solution)/shard_map/out_dot/pallas_call | solution.py:357
  367.5 3.1 copy.6
Async XLA Ops:
  171.0 0.7 copy-start
  171.7 1.6 copy-start.1
  207.1 1.3 copy-start.2

commit v2 on v1

--- a/solution.py
+++ b/solution.py
@@ -366,6 +366,234 @@
     )(x, w, seg)
 
 
+def _out_dot(x_hbm, w_hbm, y_hbm, xg, wg, wg2, y1, y2, loc, w_send, w_recv, o_send, o_recv, e_send, e_recv, y_send, y_recv):
+    R, C = x_hbm.shape
+    N = w_hbm.shape[1]
+    RC, NH = R // NR, N // (2 * NP)
+    d, t, s = lax.axis_index("dp"), lax.axis_index("tp"), lax.axis_index("sp")
+    yc, c = s // 2, s % 2
+    sib, ynb, diag = s + 1 - 2 * c, s + 2 - 4 * yc, (2 - 2 * yc) + (1 - c)
+    mesh_id = pl.DeviceIdType.MESH
+    to_sib, to_y, to_x = (d, t, sib), (d, t, ynb), (1 - d, t, s)
+    is_end = (t == 0) | (t == NT - 1)
+    bar = pltpu.get_barrier_semaphore()
+
+    def greet(who):
+        pl.semaphore_signal(bar, inc=1, device_id=who, device_id_type=mesh_id)
+
+    def remote(src, dst, send, recv, who):
+        return pltpu.make_async_remote_copy(src, dst, send, recv, device_id=who, device_id_type=mesh_id)
+
+    def rows(r):
+        return pl.ds(_mo(r, RC), RC)
+
+    def mine(p):
+        return pl.ds(_mo(2 * p + d, NH), NH)
+
+    def other(p):
+        return pl.ds(_mo(2 * p + 1 - d, NH), NH)
+
+    kinds = {
+        "y2": (wg2, s, mine, to_y, ynb, mine),
+        "xo2": (wg2, s, mine, to_x, s, other),
+        "so2": (wg2, s, mine, to_sib, sib, mine),
+        "x2": (wg2, ynb, mine, to_x, ynb, other),
+        "sy2": (wg2, ynb, mine, to_sib, diag, mine),
+        "sx2": (wg2, s, other, to_sib, sib, other),
+        "sxy2": (wg2, ynb, other, to_sib, diag, other),
+        "y1": (wg, s, mine, to_y, ynb, mine),
+        "x1": (wg, ynb, mine, to_x, ynb, other),
+        "sy1": (wg, ynb, mine, to_sib, diag, mine),
+        "sx1": (wg, ynb, other, to_sib, diag, other),
+    }
+    number = {kind: i for i, kind in enumerate(kinds)}
+
+    def w_out(kind, p):
+        panel, owner, cols, who, _, _ = kinds[kind]
+        n = number[kind]
+        src = w_hbm.at[:, cols(p)] if kind == "y1" else panel.at[owner, :, cols(p)]
+        return remote(src, panel.at[owner, :, cols(p)], w_send.at[n, p], w_recv.at[n, p], who)
+
+    def w_in(kind, p):
+        panel, _, _, who, owner, cols = kinds[kind]
+        n = number[kind]
+        at = panel.at[owner, :, cols(p)]
+        return remote(at, at, w_send.at[n, p], w_recv.at[n, p], who)
+
+    @pl.when(is_end)
+    def _():
+        m = (t + 3) // 3
+        to_m = (d, m, s)
+        greet(to_m)
+        pl.semaphore_wait(bar, 1)
+
+        def w_z(p):
+            return remote(w_hbm.at[:, mine(p)], wg2.at[s, :, mine(p)], e_send.at[0, p], e_recv.at[0, p], to_m)
+
+        def x_z(r):
+            return remote(x_hbm.at[rows(r)], xg.at[t, rows(r)], e_send.at[1, r], e_recv.at[1, r], to_m)
+
+        for p in range(NP):
+            w_z(p).start()
+        for r in range(NR):
+            x_z(r).start()
+        for p in range(NP):
+            w_z(p).wait_send()
+        for r in range(NR):
+            x_z(r).wait_send()
+        for r in range(NR):
+            remote(y_hbm.at[rows(r)], y_hbm.at[rows(r)], y_send.at[r], y_recv.at[r], to_m).wait_recv()
+
+    @pl.when(jnp.logical_not(is_end))
+    def _():
+        e, o = 3 * t - 3, 3 - t
+        oe = 3 - e
+        to_e, to_o = (d, e, s), (d, o, s)
+        for who in (to_e, to_o, to_y, to_x, to_sib):
+            greet(who)
+        pl.semaphore_wait(bar, 5)
+
+        def x_own(r):
+            return remote(x_hbm.at[rows(r)], xg.at[t, rows(r)], o_send.at[0, r], o_recv.at[0, r], to_o)
+
+        def x_end(r):
+            return remote(xg.at[e, rows(r)], xg.at[e, rows(r)], o_send.at[1, r], o_recv.at[1, r], to_o)
+
+        def x_in(i, r):
+            k = o if i == 0 else oe
+            return remote(xg.at[k, rows(r)], xg.at[k, rows(r)], o_send.at[i, r], o_recv.at[i, r], to_o)
+
+        def relay_end(r):
+            remote(xg.at[e, rows(r)], xg.at[e, rows(r)], e_send.at[1, r], e_recv.at[1, r], to_e).wait_recv()
+            x_end(r).start()
+
+        own_x = pltpu.make_async_copy(x_hbm, xg.at[t], loc.at[0])
+        own_w = pltpu.make_async_copy(w_hbm, wg.at[s], loc.at[1])
+        w_so1 = remote(w_hbm, wg.at[s], loc.at[2], loc.at[3], to_sib)
+        w_so1_in = remote(w_hbm, wg.at[sib], loc.at[2], loc.at[3], to_sib)
+        for r in range(NR):
+            x_own(r).start()
+        own_x.start()
+        own_w.start()
+        w_so1.start()
+
+        for i in range(NR + NP):
+            if i < NP:
+                at = wg2.at[s, :, mine(i)]
+                remote(at, at, e_send.at[0, i], e_recv.at[0, i], to_e).wait_recv()
+                w_out("y2", i).start()
+                w_out("xo2", i).start()
+                w_out("so2", i).start()
+            if i == NP - 1:
+                for p in range(NP):
+                    w_out("y1", p).start()
+            if 1 <= i <= NP:
+                w_in("y2", i - 1).wait_recv()
+                w_out("x2", i - 1).start()
+                w_out("sy2", i - 1).start()
+            if i >= NP:
+                relay_end(i - NP)
+                if i < 2 * NP:
+                    w_in("y1", i - NP).wait_recv()
+                    w_out("x1", i - NP).start()
+                    w_out("sy1", i - NP).start()
+                    w_in("xo2", i - NP).wait_recv()
+                    w_out("sx2", i - NP).start()
+                else:
+                    w_in("x2", i - 2 * NP).wait_recv()
+                    w_out("sxy2", i - 2 * NP).start()
+        for kind in ("so2", "sy2", "sx2", "sxy2"):
+            for p in range(NP):
+                w_in(kind, p).wait_recv()
+        own_x.wait()
+
+        def unit(panel, out, r):
+            acc = jnp.dot(xg[0, rows(r), :], panel[0], preferred_element_type=jnp.float32)
+            for k in range(1, NT):
+                acc += jnp.dot(xg[k, rows(r), :], panel[k], preferred_element_type=jnp.float32)
+            out[rows(r), :] = acc.astype(jnp.bfloat16)
+
+        def y_out(r):
+            return remote(y2.at[rows(r)], y_hbm.at[rows(r)], y_send.at[r], y_recv.at[r], to_e)
+
+        def first(r, z):
+            x_in(0, r).wait_recv()
+            x_in(1, r).wait_recv()
+            unit(wg2, y2, r)
+
+            @pl.when(r > 0)
+            def _():
+                y_out(r - 1).start()
+
+            return z
+
+        half = NR // 2
+        lax.fori_loop(0, half, first, 0)
+        y_out(half - 1).start()
+        for p in range(NP):
+            w_in("x1", p).wait_recv()
+            w_out("sx1", p).start()
+        own_w.wait()
+        w_so1_in.wait_recv()
+        for kind in ("sy1", "sx1"):
+            for p in range(NP):
+                w_in(kind, p).wait_recv()
+
+        def second(r, z):
+            x_in(0, r).wait_recv()
+            x_in(1, r).wait_recv()
+            unit(wg2, y2, r)
+
+            def own(i, z):
+                unit(wg, y1, 2 * (r - half) + i)
+
+                @pl.when(i == 0)
+                def _():
+                    y_out(r).start()
+
+                return z
+
+            return lax.fori_loop(0, 2, own, z)
+
+        lax.fori_loop(half, NR, second, 0)
+        own_y = pltpu.make_async_copy(y1, y_hbm, loc.at[0])
+        own_y.start()
+        w_so1.wait_send()
+        for r in range(NR):
+            x_own(r).wait_send()
+            x_end(r).wait_send()
+            y_out(r).wait_send()
+        for kind in kinds:
+            for p in range(NP):
+                w_out(kind, p).wait_send()
+        own_y.wait()
+
+
+def _out_call(x, w):
+    R, C = x.shape
+    N = w.shape[1]
+    dma = pltpu.SemaphoreType.DMA
+    hbm = pl.BlockSpec(memory_space=pltpu.HBM)
+    bf16 = jnp.bfloat16
+    return pl.pallas_call(
+        _out_dot,
+        out_shape=jax.ShapeDtypeStruct((R, N), bf16),
+        in_specs=[hbm, hbm],
+        out_specs=hbm,
+        scratch_shapes=[
+            pltpu.VMEM((NT, R, C), bf16),
+            pltpu.VMEM((NT, C, N), bf16),
+            pltpu.VMEM((NT, C, N), bf16),
+            pltpu.VMEM((R, N), bf16),
+            pltpu.VMEM((R, N), bf16),
+            dma((4,)), dma((11, NP)), dma((11, NP)), dma((2, NR)), dma((2, NR)), dma((2, NR)), dma((2, NR)), dma((NR,)), dma((NR,)),
+        ],
+        compiler_params=pltpu.CompilerParams(collective_id=1, has_side_effects=True, vmem_limit_bytes=60 * MIB),
+        cost_estimate=pl.CostEstimate(flops=4 * R * NT * C * N, bytes_accessed=2 * NT * (R * C + C * N), transcendentals=0),
+        name="out_dot",
+    )(x, w)
+
+
 def _attention(BQ, BK, s_ref, seg_ref, q_ref, kv_ref, o_ref, st_ref, sc_ref, m_ref, l_ref, acc_ref):
     R = q_ref.shape[0]
     s = s_ref[0]
@@ -483,7 +711,7 @@
         seg = seg_blk.reshape(-1, 128)
         q, kv_all, seg_all = _gather_call(True, x_blk, wqkv_blk, seg)
         context = _attention_call(q, kv_all.reshape(NT * R, -1), seg_all.reshape(-1, 128))
-        return _gather_call(False, context, wout_blk, seg)
+        return _out_call(context, wout_blk)
 
     row_spec = P(("dp", "sp"), "tp")
     return jax.shard_map(local_block, mesh=mesh, in_specs=(row_spec, P("sp", "tp"), P("sp", "tp"), P(("dp", "sp"))), out_specs=row_spec, check_vma=False)

time: 376 us -> 337 us (0.90)
  the two profiles are of different devices: /device:TPU:4 before, /device:TPU:7 now
where the time goes in v2:
time: 337 us; the launch traced here: 336 us
  Pallas kernels  329 us (98%)
  local copies, waits for them, and re-layouts  6.7 us (2%)
    pallas_call x1, Pallas kernels, _gather_call(): pl.pallas_call(functools.partial(_gather_dot, qkv), out_shape=out_shape,...  170 us
    pallas_call x1, Pallas kernels, _out_call(): pl.pallas_call(_out_dot, out_shape=jax.ShapeDtypeStruct((R, N), bf16), in...  116 us
    pallas_call x1, Pallas kernels, _attention_call(): pl.pallas_call(functools.partial(_attention, BQ, BK), out_shape=jax.Shape...  43.6 us

profile of v2, /device:TPU:7, one launch (start us, length us, event | category | flops | bytes accessed | tf_op | source)
XLA Modules:
  0.0 336.2 jit_solution(16078990706454261420)
XLA Ops:
  0.0 170.2 %qkv_dot.1 = (bf16[1024,1024]{1,0:T(8,128)(2,1)}, bf16[4,1024,2048]{2,1,0:T(8,128)(2,1)}, s32[4,8,128]{2,1,0:T(8,128)}) custom-call(bf16[1024,1024]{1,0:T(8,128)(2,1)} %x_hbm.1, bf16[1024,3072]{1,0:T(8,128)(2,1)} %w_hbm.2, s32[8,128]{1,0:T(8,128)} %bitcast.5), custom_call_target="tpu_custom_call" | custom-call | flops 25769803776 | bytes 33554432 | tf_op jit(solution)/shard_map/qkv_dot/pallas_call | solution.py:357
  170.2 0.0 copy-start
  170.2 0.7 copy-done
  170.9 0.0 copy-start.1
  170.9 1.6 copy-done.1
  172.5 43.6 %attention.1.x_hbm = bf16[1024,1024]{1,0:T(8,128)(2,1)S(1)} custom-call(s32[1]{0:T(128)} %bitcast.s_ref, s32[32,128]{1,0:T(8,128)S(1)} %bitcast.4, bf16[1024,1024]{1,0:T(8,128)(2,1)S(1)} %copy-done.1, bf16[4096,2048]{1,0:T(8,128)(2,1)} %bitcast.6), custom_call_target="tpu_custom_call" | custom-call | flops 8589934592 | bytes 16777216 | tf_op jit(solution)/shard_map/attention/pallas_call | solution.py:682
  216.1 0.0 copy-start.2
  216.1 1.3 copy-done.2
  217.4 115.7 %out_dot.1 = bf16[1024,1024]{1,0:T(8,128)(2,1)} custom-call(bf16[1024,1024]{1,0:T(8,128)(2,1)} %copy-done.2, bf16[1024,1024]{1,0:T(8,128)(2,1)} %w_hbm.3), custom_call_target="tpu_custom_call" | custom-call | flops 17179869184 | bytes 16777216 | tf_op jit(solution)/shard_map/out_dot/pallas_call | solution.py:578
  333.1 3.1 copy.6
Async XLA Ops:
  170.2 0.7 copy-start
  170.9 1.6 copy-start.1
  216.1 1.3 copy-start.2

commit v3 on v1

--- a/solution.py
+++ b/solution.py
@@ -10,6 +10,7 @@
 HEAD_DIM = 128
 NT = 4
 NR = 8
+NB = 4
 NP = 4
 LOG2E = 1.4426950408889634
 MIB = 1024 * 1024
@@ -366,20 +367,141 @@
     )(x, w, seg)
 
 
-def _attention(BQ, BK, s_ref, seg_ref, q_ref, kv_ref, o_ref, st_ref, sc_ref, m_ref, l_ref, acc_ref):
-    R = q_ref.shape[0]
-    s = s_ref[0]
+def _attend_out(q_hbm, kv_hbm, seg_hbm, w_hbm, y_hbm, q_ref, kv_ref, seg_ref, first_ref, sc_ref, m_ref, l_ref, acc_ref, xg, wg, wg2, y1, y2,
+                loc, kv_sem, w_send, w_recv, o_send, o_recv, e_send, e_recv, z_send, z_recv, y_send, y_recv):
+    R, C = q_hbm.shape
+    N = w_hbm.shape[1]
+    RC, NH = R // NR, N // (2 * NP)
+    BQ = R // NB
+    BK = 2 * BQ
+    CP = 2 * HEAD_DIM
+    NU = NB * (C // CP)
+    d, t, s = lax.axis_index("dp"), lax.axis_index("tp"), lax.axis_index("sp")
+    yc, c = s // 2, s % 2
+    sib, ynb, diag = s + 1 - 2 * c, s + 2 - 4 * yc, (2 - 2 * yc) + (1 - c)
+    mesh_id = pl.DeviceIdType.MESH
+    to_sib, to_y, to_x = (d, t, sib), (d, t, ynb), (1 - d, t, s)
+    is_end = (t == 0) | (t == NT - 1)
+    is_mid = jnp.logical_not(is_end)
+    e, o = 3 * t - 3, 3 - t
+    oe = 3 - e
+    m_plane = (t + 3) // 3
+    to_m, to_e, to_o = (d, m_plane, s), (d, e, s), (d, o, s)
+    bar = pltpu.get_barrier_semaphore()
+
+    def greet(who):
+        pl.semaphore_signal(bar, inc=1, device_id=who, device_id_type=mesh_id)
+
+    def remote(src, dst, send, recv, who):
+        return pltpu.make_async_remote_copy(src, dst, send, recv, device_id=who, device_id_type=mesh_id)
+
+    def rows(r):
+        return pl.ds(_mo(r, RC), RC)
+
+    def mine(p):
+        return pl.ds(_mo(2 * p + d, NH), NH)
+
+    def other(p):
+        return pl.ds(_mo(2 * p + 1 - d, NH), NH)
+
+    def piece(k, u):
+        return xg.at[k, pl.ds(_mo(u // (C // CP), BQ), BQ), pl.ds(_mo(u % (C // CP), CP), CP)]
+
+    kinds = {
+        "y2": (wg2, s, mine, to_y, ynb, mine),
+        "xo2": (wg2, s, mine, to_x, s, other),
+        "so2": (wg2, s, mine, to_sib, sib, mine),
+        "x2": (wg2, ynb, mine, to_x, ynb, other),
+        "sy2": (wg2, ynb, mine, to_sib, diag, mine),
+        "sx2": (wg2, s, other, to_sib, sib, other),
+        "sxy2": (wg2, ynb, other, to_sib, diag, other),
+        "y1": (wg, s, mine, to_y, ynb, mine),
+        "x1": (wg, ynb, mine, to_x, ynb, other),
+        "sy1": (wg, ynb, mine, to_sib, diag, mine),
+        "sx1": (wg, ynb, other, to_sib, diag, other),
+    }
+    number = {kind: i for i, kind in enumerate(kinds)}
+
+    def w_out(kind, p):
+        panel, owner, cols, who, _, _ = kinds[kind]
+        n = number[kind]
+        src = w_hbm.at[:, cols(p)] if kind == "y1" else panel.at[owner, :, cols(p)]
+        return remote(src, panel.at[owner, :, cols(p)], w_send.at[n, p], w_recv.at[n, p], who)
+
+    def w_in(kind, p):
+        panel, _, _, who, owner, cols = kinds[kind]
+        n = number[kind]
+        at = panel.at[owner, :, cols(p)]
+        return remote(at, at, w_send.at[n, p], w_recv.at[n, p], who)
+
+    def w_z(p, who):
+        return remote(w_hbm.at[:, mine(p)], wg2.at[s, :, mine(p)], z_send.at[p], z_recv.at[p], who)
+
+    def end_piece(u, who):
+        k = t if who is to_m else e
+        return remote(piece(k, u), piece(k, u), e_send.at[u], e_recv.at[u], who)
+
+    def own_piece(u):
+        return remote(piece(t, u), piece(t, u), o_send.at[0, u], o_recv.at[0, u], to_o)
+
+    def passed_piece(u):
+        return remote(piece(e, u), piece(e, u), o_send.at[1, u], o_recv.at[1, u], to_o)
+
+    def piece_in(i, u):
+        k = o if i == 0 else oe
+        return remote(piece(k, u), piece(k, u), o_send.at[i, u], o_recv.at[i, u], to_o)
+
+    def y_out(r, who):
+        return remote(y2.at[rows(r)], y_hbm.at[rows(r)], y_send.at[r], y_recv.at[r], who)
+
+    q_copy = pltpu.make_async_copy(q_hbm, q_ref, loc.at[0])
+    seg_copy = pltpu.make_async_copy(seg_hbm, seg_ref, loc.at[1])
+    own_w = pltpu.make_async_copy(w_hbm, wg.at[s], loc.at[2])
+
+    def kv_copy(g, k):
+        return pltpu.make_async_copy(kv_hbm.at[k, :, pl.ds(_mo(g, 2 * CP), 2 * CP)], kv_ref.at[g, pl.ds(_mo(k, R), R)], kv_sem.at[g, k])
+
+    w_so1 = remote(w_hbm, wg.at[s], loc.at[3], loc.at[4], to_sib)
+    w_so1_in = remote(w_hbm, wg.at[sib], loc.at[3], loc.at[4], to_sib)
+    seg_copy.start()
+    q_copy.start()
+    for g in range(C // CP):
+        for k in range(NT):
+            @pl.when(k <= s)
+            def _():
+                kv_copy(g, k).start()
+
+    @pl.when(is_end)
+    def _():
+        greet(to_m)
+        pl.semaphore_wait(bar, 1)
+        for p in range(NP):
+            w_z(p, to_m).start()
+
+    @pl.when(is_mid)
+    def _():
+        for who in (to_e, to_o, to_y, to_x, to_sib):
+            greet(who)
+        pl.semaphore_wait(bar, 5)
+        own_w.start()
+        w_so1.start()
+
+    seg_copy.wait()
     seg = seg_ref[...]
+    starts = [jnp.sum(jnp.where(seg < doc, 1.0, 0.0), axis=(0, 1), keepdims=True) for doc in range(1, 4)]
+
+    def first_rows(b, z):
+        row = (s * R + b * BQ + lax.broadcasted_iota(jnp.int32, (BQ, HEAD_DIM), 0)).astype(jnp.float32)
+        out = jnp.zeros((BQ, HEAD_DIM), jnp.float32)
+        for start in starts:
+            out = jnp.where(start <= row, jnp.maximum(out, start), out)
+        first_ref[pl.ds(_mo(b, BQ), BQ), :] = out.astype(jnp.int32)
+        return z
+
+    lax.fori_loop(0, NB, first_rows, 0)
+    q_copy.wait()
+
     scale = LOG2E / HEAD_DIM ** 0.5
-    for doc in range(1, 4):
-        st_ref[doc] = jnp.sum((seg < doc).astype(jnp.int32))
-
-    def doc_start(row):
-        out = jnp.zeros_like(row)
-        for doc in range(1, 4):
-            start = st_ref[doc]
-            out = jnp.where(start <= row, jnp.maximum(out, start), out)
-        return out
 
     def lane_groups(a, op):
         out = a[:, :HEAD_DIM]
@@ -387,103 +509,241 @@
             out = op(out, a[:, HEAD_DIM * g : HEAD_DIM * (g + 1)])
         return out
 
-    def q_block(b, z):
-        row0 = s * R + b * BQ
+    def wide(a):
+        return jnp.concatenate([a] * (BK // HEAD_DIM), axis=1)
+
+    def attend(u):
+        b, g = u // (C // CP), u % (C // CP)
         q_at = pl.ds(_mo(b, BQ), BQ)
-        lo = doc_start(row0) // BK
-        hi = (row0 + BQ - 1) // BK + 1
-        full_lo = jnp.clip((doc_start(row0 + BQ - 1) + BK - 1) // BK, lo, hi)
-        full_hi = jnp.clip((row0 + 1) // BK, full_lo, hi)
+        full = (s * R) // BK + b // 2
         m_ref[...] = jnp.full(m_ref.shape, -3e38, jnp.float32)
         l_ref[...] = jnp.zeros(l_ref.shape, jnp.float32)
         acc_ref[...] = jnp.zeros(acc_ref.shape, jnp.float32)
 
-        def scores(j, z, masked):
+        def scores(j, z, diagonal):
             k_at = pl.ds(_mo(j, BK), BK)
-            if masked:
-                row_id = row0 + lax.broadcasted_iota(jnp.int32, (BQ, 1), 0)
-                key_id = j * BK + lax.broadcasted_iota(jnp.int32, (BQ, BK), 1)
-                seen = (key_id <= row_id) & (key_id >= doc_start(row_id))
+            key_id = j * BK + lax.broadcasted_iota(jnp.int32, (BQ, BK), 1)
+            seen = key_id >= wide(first_ref[q_at, :])
+            if diagonal:
+                seen = seen & (key_id <= s * R + b * BQ + lax.broadcasted_iota(jnp.int32, (BQ, BK), 0))
             for h in range(2):
-                q = q_ref[q_at, HEAD_DIM * h : HEAD_DIM * (h + 1)]
-                k = kv_ref[k_at, 2 * HEAD_DIM * h : 2 * HEAD_DIM * h + HEAD_DIM]
+                q = q_ref[q_at, pl.ds(pl.multiple_of(g * CP + h * HEAD_DIM, HEAD_DIM), HEAD_DIM)]
+                k = kv_ref[g, k_at, 2 * HEAD_DIM * h : 2 * HEAD_DIM * h + HEAD_DIM]
                 sc = lax.dot_general(q, k, (((1,), (1,)), ((), ())), preferred_element_type=jnp.float32)
-                if masked:
-                    sc = jnp.where(seen, sc, -jnp.inf)
+                sc = jnp.where(seen, sc, -jnp.inf)
                 sc_ref[h, j] = sc
                 m_ref[h] = jnp.maximum(m_ref[h], lane_groups(sc, jnp.maximum))
             return z
 
         def weights(j, z):
             for h in range(2):
-                m = m_ref[h]
-                e = jnp.exp2((sc_ref[h, j] - jnp.concatenate([m] * (BK // HEAD_DIM), axis=1)) * scale)
-                sc_ref[h, j] = e
-                l_ref[h] = l_ref[h] + lane_groups(e, jnp.add)
+                p = jnp.exp2((sc_ref[h, j] - wide(m_ref[h])) * scale)
+                sc_ref[h, j] = p
+                l_ref[h] = l_ref[h] + lane_groups(p, jnp.add)
             return z
 
         def values(j, z):
             k_at = pl.ds(_mo(j, BK), BK)
             for h in range(2):
-                v = kv_ref[k_at, 2 * HEAD_DIM * h + HEAD_DIM : 2 * HEAD_DIM * (h + 1)]
-                p = (sc_ref[h, j] * jnp.concatenate([l_ref[h]] * (BK // HEAD_DIM), axis=1)).astype(jnp.bfloat16)
+                v = kv_ref[g, k_at, 2 * HEAD_DIM * h + HEAD_DIM : 2 * HEAD_DIM * (h + 1)]
+                p = (sc_ref[h, j] * wide(l_ref[h])).astype(jnp.bfloat16)
                 acc_ref[h] = acc_ref[h] + jnp.dot(p, v, preferred_element_type=jnp.float32)
             return z
 
-        lax.fori_loop(lo, full_lo, functools.partial(scores, masked=True), 0)
-        lax.fori_loop(full_lo, full_hi, functools.partial(scores, masked=False), 0)
-        lax.fori_loop(full_hi, hi, functools.partial(scores, masked=True), 0)
+        lax.fori_loop(0, full, functools.partial(scores, diagonal=False), 0)
+        scores(full, 0, True)
         for h in range(2):
             m_ref[h] = jnp.broadcast_to(jnp.max(m_ref[h], axis=1, keepdims=True), (BQ, HEAD_DIM))
-        lax.fori_loop(lo, hi, weights, 0)
+        lax.fori_loop(0, full + 1, weights, 0)
         for h in range(2):
             l_ref[h] = jnp.broadcast_to(1.0 / jnp.sum(l_ref[h], axis=1, keepdims=True), (BQ, HEAD_DIM))
-        lax.fori_loop(lo, hi, values, 0)
+        lax.fori_loop(0, full + 1, values, 0)
         for h in range(2):
-            o_ref[q_at, HEAD_DIM * h : HEAD_DIM * (h + 1)] = acc_ref[h].astype(jnp.bfloat16)
+            xg[t, q_at, pl.ds(pl.multiple_of(g * CP + h * HEAD_DIM, HEAD_DIM), HEAD_DIM)] = acc_ref[h].astype(jnp.bfloat16)
+
+    def dot_rows(panel, out, r):
+        acc = jnp.dot(xg[0, rows(r), :], panel[0], preferred_element_type=jnp.float32)
+        for k in range(1, NT):
+            acc += jnp.dot(xg[k, rows(r), :], panel[k], preferred_element_type=jnp.float32)
+        out[rows(r), :] = acc.astype(jnp.bfloat16)
+
+    def project(lo, hi):
+        def chunk(r, z):
+            dot_rows(wg2, y2, r)
+            dot_rows(wg, y1, r)
+            y_out(r, to_e).start()
+            return z
+
+        lax.fori_loop(lo, hi, chunk, 0)
+
+    def pieces_in(lo, hi):
+        def wait(u, z):
+            piece_in(0, u).wait_recv()
+            piece_in(1, u).wait_recv()
+            return z
+
+        lax.fori_loop(lo, hi, wait, 0)
+
+    def relay_piece(u):
+        end_piece(u, to_e).wait_recv()
+        passed_piece(u).start()
+
+    def relay_w(u):
+        @pl.when(u < NP)
+        def _():
+            w_z(u, to_e).wait_recv()
+            w_out("y2", u).start()
+            w_out("xo2", u).start()
+            w_out("so2", u).start()
+
+        @pl.when(u == NP - 1)
+        def _():
+            for p in range(NP):
+                w_out("y1", p).start()
+
+        @pl.when((u >= 1) & (u <= NP))
+        def _():
+            w_in("y2", u - 1).wait_recv()
+            w_out("x2", u - 1).start()
+            w_out("sy2", u - 1).start()
+
+        @pl.when((u >= NP) & (u < 2 * NP))
+        def _():
+            p = u - NP
+            w_in("y1", p).wait_recv()
+            w_out("x1", p).start()
+            w_out("sy1", p).start()
+            w_in("xo2", p).wait_recv()
+            w_out("sx2", p).start()
+
+        @pl.when((u >= 2 * NP) & (u < 3 * NP))
+        def _():
+            p = u - 2 * NP
+            w_in("x2", p).wait_recv()
+            w_out("sxy2", p).start()
+            w_in("x1", p).wait_recv()
+            w_out("sx1", p).start()
+
+        @pl.when(u == 3 * NP - 1)
+        def _():
+            own_w.wait()
+            w_so1_in.wait_recv()
+            for kind in ("so2", "sy2", "sx2", "sxy2", "sy1", "sx1"):
+                for p in range(NP):
+                    w_in(kind, p).wait_recv()
+
+    per = C // CP
+    cb = BQ // RC
+
+    def step(u, z):
+        @pl.when(u < per)
+        def _():
+            for k in range(NT):
+                @pl.when(k <= s)
+                def _():
+                    kv_copy(u, k).wait()
+
+        attend(u)
+
+        @pl.when(is_end)
+        def _():
+            end_piece(u, to_m).start()
+
+        @pl.when(is_mid)
+        def _():
+            relay_w(u)
+
+            @pl.when(u >= 1)
+            def _():
+                relay_piece(u - 1)
+
+            own_piece(u).start()
+
+            @pl.when((u == NU - 5) | (u == NU - 2))
+            def _():
+                late = (u - (NU - 5)) // 3
+                pieces_in(late * 2 * per, 2 * per + late * per)
+                project(late * 2 * cb, 2 * cb + late * cb)
+
         return z
 
-    lax.fori_loop(0, R // BQ, q_block, 0)
-
-
-def _attention_call(q, kv_all, seg_all):
-    R, cols = q.shape
-    rows = NT * R
-    BQ, BK = min(512, R), min(512, R)
-    s = lax.axis_index("sp").astype(jnp.int32).reshape(1)
+    lax.fori_loop(0, NU, step, 0)
+
+    @pl.when(is_end)
+    def _():
+        for p in range(NP):
+            w_z(p, to_m).wait_send()
+
+        def drain(u, z):
+            end_piece(u, to_m).wait_send()
+            return z
+
+        lax.fori_loop(0, NU, drain, 0)
+        for r in range(NR):
+            y_out(r, to_m).wait_recv()
+
+    @pl.when(is_mid)
+    def _():
+        relay_piece(NU - 1)
+        pieces_in(3 * per, NU)
+        project(3 * cb, NR)
+        own_y = pltpu.make_async_copy(y1, y_hbm, loc.at[0])
+        own_y.start()
+        w_so1.wait_send()
+
+        def drain(u, z):
+            own_piece(u).wait_send()
+            passed_piece(u).wait_send()
+            return z
+
+        lax.fori_loop(0, NU, drain, 0)
+        for r in range(NR):
+            y_out(r, to_e).wait_send()
+        for kind in kinds:
+            for p in range(NP):
+                w_out(kind, p).wait_send()
+        own_y.wait()
+
+
+def _attend_call(q, kv_all, seg_all, w):
+    R, C = q.shape
+    N = w.shape[1]
+    BQ = R // NB
+    NU = NB * (C // (2 * HEAD_DIM))
+    dma = pltpu.SemaphoreType.DMA
+    hbm = pl.BlockSpec(memory_space=pltpu.HBM)
+    bf16, f32 = jnp.bfloat16, jnp.float32
+    stat = pltpu.VMEM((2, BQ, HEAD_DIM), f32)
     return pl.pallas_call(
-        functools.partial(_attention, BQ, BK),
-        out_shape=jax.ShapeDtypeStruct((R, cols), jnp.bfloat16),
-        grid_spec=pltpu.PrefetchScalarGridSpec(
-            num_scalar_prefetch=1,
-            grid=(cols // (2 * HEAD_DIM),),
-            in_specs=[
-                pl.BlockSpec(seg_all.shape, lambda p, s: (0, 0)),
-                pl.BlockSpec((R, 2 * HEAD_DIM), lambda p, s: (0, p)),
-                pl.BlockSpec((rows, 4 * HEAD_DIM), lambda p, s: (0, p)),
-            ],
-            out_specs=pl.BlockSpec((R, 2 * HEAD_DIM), lambda p, s: (0, p)),
-            scratch_shapes=[
-                pltpu.SMEM((4,), jnp.int32),
-                pltpu.VMEM((2, rows // BK, BQ, BK), jnp.float32),
-                pltpu.VMEM((2, BQ, HEAD_DIM), jnp.float32),
-                pltpu.VMEM((2, BQ, HEAD_DIM), jnp.float32),
-                pltpu.VMEM((2, BQ, HEAD_DIM), jnp.float32),
-            ],
-        ),
-        compiler_params=pltpu.CompilerParams(vmem_limit_bytes=48 * MIB),
-        cost_estimate=pl.CostEstimate(flops=2 * R * rows * cols, bytes_accessed=4 * rows * cols, transcendentals=R * rows * cols // 256),
-        name="attention",
-    )(s, seg_all, q, kv_all)
+        _attend_out,
+        out_shape=jax.ShapeDtypeStruct((R, N), bf16),
+        in_specs=[hbm] * 4,
+        out_specs=hbm,
+        scratch_shapes=[
+            pltpu.VMEM((R, C), bf16),
+            pltpu.VMEM((C // (2 * HEAD_DIM), NT * R, 4 * HEAD_DIM), bf16),
+            pltpu.VMEM(seg_all.shape, jnp.int32),
+            pltpu.VMEM((R, HEAD_DIM), jnp.int32),
+            pltpu.VMEM((2, NT * NB // 2, BQ, 2 * BQ), f32),
+            stat, stat, stat,
+            pltpu.VMEM((NT, R, C), bf16),
+            pltpu.VMEM((NT, C, N), bf16),
+            pltpu.VMEM((NT, C, N), bf16),
+            pltpu.VMEM((R, N), bf16),
+            pltpu.VMEM((R, N), bf16),
+            dma((5,)), dma((C // (2 * HEAD_DIM), NT)), dma((11, NP)), dma((11, NP)), dma((2, NU)), dma((2, NU)), dma((NU,)), dma((NU,)),
+            dma((NP,)), dma((NP,)), dma((NR,)), dma((NR,)),
+        ],
+        compiler_params=pltpu.CompilerParams(collective_id=1, has_side_effects=True, vmem_limit_bytes=62 * MIB),
+        cost_estimate=pl.CostEstimate(flops=4 * R * NT * C * N, bytes_accessed=2 * NT * (R * C + C * N), transcendentals=R * NT * R * 4),
+        name="attend_out",
+    )(q, kv_all, seg_all, w)
 
 
 def solution(mesh):
     def local_block(x_blk, wqkv_blk, wout_blk, seg_blk):
-        R = x_blk.shape[0]
-        seg = seg_blk.reshape(-1, 128)
-        q, kv_all, seg_all = _gather_call(True, x_blk, wqkv_blk, seg)
-        context = _attention_call(q, kv_all.reshape(NT * R, -1), seg_all.reshape(-1, 128))
-        return _gather_call(False, context, wout_blk, seg)
+        q, kv_all, seg_all = _gather_call(True, x_blk, wqkv_blk, seg_blk.reshape(-1, 128))
+        return _attend_call(q, kv_all, seg_all.reshape(-1, 128), wout_blk)
 
     row_spec = P(("dp", "sp"), "tp")
     return jax.shard_map(local_block, mesh=mesh, in_specs=(row_spec, P("sp", "tp"), P("sp", "tp"), P(("dp", "sp"))), out_specs=row_spec, check_vma=False)

time: 376 us -> 324 us (0.86)
  the two profiles are of different devices: /device:TPU:4 before, /device:TPU:7 now
where the time goes in v3:
time: 324 us; the launch traced here: 323 us
  Pallas kernels  320 us (99%)
    pallas_call x1, Pallas kernels, _gather_call(): pl.pallas_call(functools.partial(_gather_dot, qkv), out_shape=out_shape,...  170 us
    pallas_call x1, Pallas kernels, _attend_call(): pl.pallas_call(_attend_out, out_shape=jax.ShapeDtypeStruct((R, N), bf16),...  150 us

profile of v3, /device:TPU:7, one launch (start us, length us, event | category | flops | bytes accessed | tf_op | source)
XLA Modules:
  0.0 323.4 jit_solution(14528435319153863730)
XLA Ops:
  0.0 170.2 %qkv_dot.1 = (bf16[1024,1024]{1,0:T(8,128)(2,1)}, bf16[4,1024,2048]{2,1,0:T(8,128)(2,1)}, s32[4,8,128]{2,1,0:T(8,128)}) custom-call(bf16[1024,1024]{1,0:T(8,128)(2,1)} %x_hbm.1, bf16[1024,3072]{1,0:T(8,128)(2,1)} %w_hbm.2, s32[8,128]{1,0:T(8,128)} %bitcast.2), custom_call_target="tpu_custom_call" | custom-call | flops 25769803776 | bytes 33554432 | tf_op jit(solution)/shard_map/qkv_dot/pallas_call | solution.py:358
  170.2 150.1 %attend_out.1 = bf16[1024,1024]{1,0:T(8,128)(2,1)} custom-call(bf16[1024,1024]{1,0:T(8,128)(2,1)} %get-tuple-element.8.q_hbm, bf16[4,1024,2048]{2,1,0:T(8,128)(2,1)} %get-tuple-element.9.kv_hbm, s32[32,128]{1,0:T(8,128)} %bitcast.3, bf16[1024,1024]{1,0:T(8,128)(2,1)} %w_hbm.3), custom_call_target="tpu_custom_call" | custom-call | flops 17179869184 | bytes 16777216 | tf_op jit(solution)/shard_map/attend_out/pallas_call | solution.py:717
  320.4 3.1 copy.6

commit v4 on v3

--- a/solution.py
+++ b/solution.py
@@ -20,10 +20,10 @@
     return pl.multiple_of(i * n, n)
 
 
-def _gather_dot(qkv, x_hbm, w_hbm, seg_hbm, *refs):
+def _gather_dot(qkv, x_hbm, w_hbm, seg_hbm, wo_hbm, *refs):
     if qkv:
-        q_ref, kv_all, seg_all = refs[:3]
-        refs = refs[3:]
+        q_ref, kv_all, seg_all, w2_hbm = refs[:4]
+        refs = refs[4:]
     else:
         (y_ref,) = refs[:1]
         refs = refs[1:]
@@ -34,7 +34,7 @@
         refs = refs[1:]
     loc, xs, xl, xr, ws_own, ws_y, ws_x, ws_f, wr_own, wr_y, wr_x, wr_f = refs[:12]
     if qkv:
-        kv_send, kv_yr, kv_cr, kv_fs, kv_fr, seg_s, seg_r = refs[12:]
+        kv_send, kv_yr, kv_cr, kv_fs, kv_fr, seg_s, seg_r, z_s, z_r, zx_s, zx_r = refs[12:]
 
     R, C = x_hbm.shape
     N = w_hbm.shape[1]
@@ -231,7 +231,30 @@
                 kv_row(r, ynb, to_y, kv_fs.at[r], kv_yr.at[r]).wait_recv()
                 kv_row(r, ynb, to_sib, kv_fs.at[r], kv_fr.at[r]).start()
 
+    is_end = (t == 0) | (t == NT - 1)
+    is_mid = jnp.logical_not(is_end)
+    N2 = wo_hbm.shape[1] // (2 * NP)
+
+    def half_cols(p, mine_cols):
+        return pl.ds(_mo(2 * p + d, N2) if mine_cols else _mo(2 * p + 1 - d, N2), N2)
+
+    def z_out(p):
+        at = half_cols(p, True)
+        return remote(wo_hbm.at[:, at], w2_hbm.at[:, at], z_s.at[p], z_r.at[p], (d, (t + 3) // 3, s))
+
+    def z_in(p):
+        at = half_cols(p, True)
+        return remote(w2_hbm.at[:, at], w2_hbm.at[:, at], z_s.at[p], z_r.at[p], to_x)
+
+    def zx(p, mine_cols):
+        at = half_cols(p, mine_cols)
+        return remote(w2_hbm.at[:, at], w2_hbm.at[:, at], zx_s.at[p], zx_r.at[p], to_x)
+
     def relay_w(i):
+        if qkv and i < NP:
+            @pl.when(is_end)
+            def _():
+                z_out(i).start()
         if i < NP:
             w_y_in(i).wait_recv()
             w_x(i).start()
@@ -267,6 +290,13 @@
 
         pass_kv(2 * (i - NP - 1))
         pass_kv(2 * (i - NP - 1) + 1)
+
+        @pl.when(is_mid & (i < NP + 3))
+        def _():
+            for p in range(2):
+                z_in(2 * (i - NP - 1) + p).wait_recv()
+                zx(2 * (i - NP - 1) + p, True).start()
+
         do_units([(NP, lambda u: (i, u))])
         return z
 
@@ -302,6 +332,18 @@
     if qkv:
         pass_kv(6)
         pass_kv(7)
+
+        @pl.when(is_end)
+        def _():
+            for p in range(NP):
+                z_out(p).wait_send()
+
+        @pl.when(is_mid)
+        def _():
+            for p in range(NP):
+                zx(p, True).wait_send()
+                zx(p, False).wait_recv()
+
         own_seg.wait()
         for i in range(3):
             seg_out(i).wait_send()
@@ -331,7 +373,7 @@
         lax.fori_loop(0, NR, drain_kv, 0)
 
 
-def _gather_call(qkv, x, w, seg):
+def _gather_call(qkv, x, w, seg, wo):
     R, C = x.shape
     N = w.shape[1]
     dma = pltpu.SemaphoreType.DMA
@@ -345,8 +387,9 @@
             jax.ShapeDtypeStruct((R, heads * HEAD_DIM), bf16),
             jax.ShapeDtypeStruct((NT, R, 2 * heads * HEAD_DIM), bf16),
             jax.ShapeDtypeStruct((NT,) + seg.shape, jnp.int32),
+            jax.ShapeDtypeStruct(wo.shape, bf16),
         )
-        out_specs = (vmem, hbm, hbm)
+        out_specs = (vmem, hbm, hbm, hbm)
         scratch.append(pltpu.VMEM((R, 2 * heads * HEAD_DIM), bf16))
     else:
         out_shape = jax.ShapeDtypeStruct((R, N), bf16)
@@ -354,28 +397,30 @@
     scratch += [dma((4,)), dma((2, 3, NR)), dma((3, NR)), dma((3, NR)), dma((NP,)), dma((NP,)), dma((NP,)), dma((2, NP)),
                 dma((NP,)), dma((NP,)), dma((NP,)), dma((2, NP))]
     if qkv:
-        scratch += [dma((2,)), dma((NR,)), dma((NR,)), dma((NR,)), dma((NR,)), dma((3,)), dma((3,))]
+        scratch += [dma((2,)), dma((NR,)), dma((NR,)), dma((NR,)), dma((NR,)), dma((3,)), dma((3,)), dma((NP,)), dma((NP,)), dma((NP,)), dma((NP,))]
     return pl.pallas_call(
         functools.partial(_gather_dot, qkv),
         out_shape=out_shape,
-        in_specs=[hbm, hbm, hbm],
+        in_specs=[hbm] * 4,
         out_specs=out_specs,
         scratch_shapes=scratch,
         compiler_params=pltpu.CompilerParams(collective_id=0 if qkv else 1, has_side_effects=True, vmem_limit_bytes=60 * MIB),
         cost_estimate=pl.CostEstimate(flops=2 * R * NT * C * N, bytes_accessed=2 * NT * (R * C + C * N), transcendentals=0),
         name="qkv_dot" if qkv else "out_dot",
-    )(x, w, seg)
-
-
-def _attend_out(q_hbm, kv_hbm, seg_hbm, w_hbm, y_hbm, q_ref, kv_ref, seg_ref, first_ref, sc_ref, m_ref, l_ref, acc_ref, xg, wg, wg2, y1, y2,
-                loc, kv_sem, w_send, w_recv, o_send, o_recv, e_send, e_recv, z_send, z_recv, y_send, y_recv):
+    )(x, w, seg, wo)
+
+
+def _attend_out(q_hbm, kv_hbm, seg_hbm, w_hbm, w2_hbm, y_hbm, q_ref, kv_ref, seg_ref, first_ref, sc0, sc1, m0, m1, l0, l1, acc_ref, xg, wg, wg2,
+                y1, y2, loc, kv_sem, w_send, w_recv, o_send, o_recv, e_send, e_recv, y_send, y_recv):
     R, C = q_hbm.shape
     N = w_hbm.shape[1]
     RC, NH = R // NR, N // (2 * NP)
     BQ = R // NB
     BK = 2 * BQ
+    H = C // HEAD_DIM
     CP = 2 * HEAD_DIM
-    NU = NB * (C // CP)
+    per = C // CP
+    NU = NB * per
     d, t, s = lax.axis_index("dp"), lax.axis_index("tp"), lax.axis_index("sp")
     yc, c = s // 2, s % 2
     sib, ynb, diag = s + 1 - 2 * c, s + 2 - 4 * yc, (2 - 2 * yc) + (1 - c)
@@ -385,8 +430,7 @@
     is_mid = jnp.logical_not(is_end)
     e, o = 3 * t - 3, 3 - t
     oe = 3 - e
-    m_plane = (t + 3) // 3
-    to_m, to_e, to_o = (d, m_plane, s), (d, e, s), (d, o, s)
+    to_m, to_e, to_o = (d, (t + 3) // 3, s), (d, e, s), (d, o, s)
     bar = pltpu.get_barrier_semaphore()
 
     def greet(who):
@@ -405,37 +449,35 @@
         return pl.ds(_mo(2 * p + 1 - d, NH), NH)
 
     def piece(k, u):
-        return xg.at[k, pl.ds(_mo(u // (C // CP), BQ), BQ), pl.ds(_mo(u % (C // CP), CP), CP)]
+        return xg.at[k, pl.ds(_mo(u // per, BQ), BQ), pl.ds(_mo(u % per, CP), CP)]
 
     kinds = {
-        "y2": (wg2, s, mine, to_y, ynb, mine),
-        "xo2": (wg2, s, mine, to_x, s, other),
-        "so2": (wg2, s, mine, to_sib, sib, mine),
-        "x2": (wg2, ynb, mine, to_x, ynb, other),
-        "sy2": (wg2, ynb, mine, to_sib, diag, mine),
-        "sx2": (wg2, s, other, to_sib, sib, other),
-        "sxy2": (wg2, ynb, other, to_sib, diag, other),
-        "y1": (wg, s, mine, to_y, ynb, mine),
-        "x1": (wg, ynb, mine, to_x, ynb, other),
-        "sy1": (wg, ynb, mine, to_sib, diag, mine),
-        "sx1": (wg, ynb, other, to_sib, diag, other),
+        "y": (s, mine, to_y, ynb, mine),
+        "x": (ynb, mine, to_x, ynb, other),
+        "sy": (ynb, mine, to_sib, diag, mine),
+        "sx": (ynb, other, to_sib, diag, other),
     }
     number = {kind: i for i, kind in enumerate(kinds)}
-
-    def w_out(kind, p):
-        panel, owner, cols, who, _, _ = kinds[kind]
+    panels = ((w_hbm, wg), (w2_hbm, wg2))
+
+    def w_out(i, kind, p):
+        hbm, panel = panels[i]
+        owner, cols, who, _, _ = kinds[kind]
         n = number[kind]
-        src = w_hbm.at[:, cols(p)] if kind == "y1" else panel.at[owner, :, cols(p)]
-        return remote(src, panel.at[owner, :, cols(p)], w_send.at[n, p], w_recv.at[n, p], who)
-
-    def w_in(kind, p):
-        panel, _, _, who, owner, cols = kinds[kind]
+        src = hbm.at[:, cols(p)] if kind == "y" else panel.at[owner, :, cols(p)]
+        return remote(src, panel.at[owner, :, cols(p)], w_send.at[i, n, p], w_recv.at[i, n, p], who)
+
+    def w_in(i, kind, p):
+        _, _, who, owner, cols = kinds[kind]
         n = number[kind]
-        at = panel.at[owner, :, cols(p)]
-        return remote(at, at, w_send.at[n, p], w_recv.at[n, p], who)
-
-    def w_z(p, who):
-        return remote(w_hbm.at[:, mine(p)], wg2.at[s, :, mine(p)], z_send.at[p], z_recv.at[p], who)
+        at = panels[i][1].at[owner, :, cols(p)]
+        return remote(at, at, w_send.at[i, n, p], w_recv.at[i, n, p], who)
+
+    def w_sib(i, owner):
+        return remote(panels[i][0], panels[i][1].at[owner], loc.at[4 + i], loc.at[6 + i], to_sib)
+
+    def w_own(i):
+        return pltpu.make_async_copy(panels[i][0], panels[i][1].at[s], loc.at[2 + i])
 
     def end_piece(u, who):
         k = t if who is to_m else e
@@ -456,35 +498,34 @@
 
     q_copy = pltpu.make_async_copy(q_hbm, q_ref, loc.at[0])
     seg_copy = pltpu.make_async_copy(seg_hbm, seg_ref, loc.at[1])
-    own_w = pltpu.make_async_copy(w_hbm, wg.at[s], loc.at[2])
-
-    def kv_copy(g, k):
-        return pltpu.make_async_copy(kv_hbm.at[k, :, pl.ds(_mo(g, 2 * CP), 2 * CP)], kv_ref.at[g, pl.ds(_mo(k, R), R)], kv_sem.at[g, k])
-
-    w_so1 = remote(w_hbm, wg.at[s], loc.at[3], loc.at[4], to_sib)
-    w_so1_in = remote(w_hbm, wg.at[sib], loc.at[3], loc.at[4], to_sib)
+
+    def kv_copy(h, k):
+        return pltpu.make_async_copy(kv_hbm.at[k, :, pl.ds(_mo(h, CP), CP)], kv_ref.at[h, pl.ds(_mo(k, R), R)], kv_sem.at[h, k])
+
     seg_copy.start()
     q_copy.start()
-    for g in range(C // CP):
+    for h in range(H):
         for k in range(NT):
             @pl.when(k <= s)
             def _():
-                kv_copy(g, k).start()
+                kv_copy(h, k).start()
 
     @pl.when(is_end)
     def _():
         greet(to_m)
         pl.semaphore_wait(bar, 1)
-        for p in range(NP):
-            w_z(p, to_m).start()
 
     @pl.when(is_mid)
     def _():
         for who in (to_e, to_o, to_y, to_x, to_sib):
             greet(who)
         pl.semaphore_wait(bar, 5)
-        own_w.start()
-        w_so1.start()
+        for i in (1, 0):
+            for p in range(NP):
+                w_out(i, "y", p).start()
+        for i in (1, 0):
+            w_sib(i, s).start()
+            w_own(i).start()
 
     seg_copy.wait()
     seg = seg_ref[...]
@@ -502,6 +543,7 @@
     q_copy.wait()
 
     scale = LOG2E / HEAD_DIM ** 0.5
+    sc, m_refs, l_refs = (sc0, sc1), (m0, m1), (l0, l1)
 
     def lane_groups(a, op):
         out = a[:, :HEAD_DIM]
@@ -512,54 +554,59 @@
     def wide(a):
         return jnp.concatenate([a] * (BK // HEAD_DIM), axis=1)
 
-    def attend(u):
-        b, g = u // (C // CP), u % (C // CP)
+    def attend(half, k, par, stages):
+        full = 2 * s + half
+        b, h = 2 * half + k // H, k % H
         q_at = pl.ds(_mo(b, BQ), BQ)
-        full = (s * R) // BK + b // 2
-        m_ref[...] = jnp.full(m_ref.shape, -3e38, jnp.float32)
-        l_ref[...] = jnp.zeros(l_ref.shape, jnp.float32)
-        acc_ref[...] = jnp.zeros(acc_ref.shape, jnp.float32)
-
-        def scores(j, z, diagonal):
-            k_at = pl.ds(_mo(j, BK), BK)
-            key_id = j * BK + lax.broadcasted_iota(jnp.int32, (BQ, BK), 1)
-            seen = key_id >= wide(first_ref[q_at, :])
-            if diagonal:
-                seen = seen & (key_id <= s * R + b * BQ + lax.broadcasted_iota(jnp.int32, (BQ, BK), 0))
-            for h in range(2):
-                q = q_ref[q_at, pl.ds(pl.multiple_of(g * CP + h * HEAD_DIM, HEAD_DIM), HEAD_DIM)]
-                k = kv_ref[g, k_at, 2 * HEAD_DIM * h : 2 * HEAD_DIM * h + HEAD_DIM]
-                sc = lax.dot_general(q, k, (((1,), (1,)), ((), ())), preferred_element_type=jnp.float32)
-                sc = jnp.where(seen, sc, -jnp.inf)
-                sc_ref[h, j] = sc
-                m_ref[h] = jnp.maximum(m_ref[h], lane_groups(sc, jnp.maximum))
+        b3, h3 = 2 * half + (k - 2) // H, (k - 2) % H
+        if 1 in stages:
+            m_refs[par][...] = jnp.full((BQ, HEAD_DIM), -3e38, jnp.float32)
+        if 2 in stages:
+            l_refs[1 - par][...] = jnp.zeros((BQ, HEAD_DIM), jnp.float32)
+        if 3 in stages:
+            acc_ref[...] = jnp.zeros((BQ, HEAD_DIM), jnp.float32)
+
+        def tile(j, z, width, diagonal):
+            if 3 in stages:
+                acc = acc_ref[...]
+                scale_l = wide(l_refs[par][...])
+                for i in range(width):
+                    p = (sc[par][j + i] * scale_l).astype(jnp.bfloat16)
+                    acc += jnp.dot(p, kv_ref[h3, pl.ds(_mo(j + i, BK), BK), HEAD_DIM:], preferred_element_type=jnp.float32)
+                acc_ref[...] = acc
+            if 1 in stages:
+                q = q_ref[q_at, pl.ds(_mo(h, HEAD_DIM), HEAD_DIM)]
+                first = wide(first_ref[q_at, :])
+                m = m_refs[par][...]
+                for i in range(width):
+                    a = lax.dot_general(q, kv_ref[h, pl.ds(_mo(j + i, BK), BK), :HEAD_DIM], (((1,), (1,)), ((), ())), preferred_element_type=jnp.float32)
+                    key_id = (j + i) * BK + lax.broadcasted_iota(jnp.int32, (BQ, BK), 1)
+                    seen = key_id >= first
+                    if diagonal:
+                        seen = seen & (key_id <= s * R + b * BQ + lax.broadcasted_iota(jnp.int32, (BQ, BK), 0))
+                    a = jnp.where(seen, a, -jnp.inf)
+                    sc[par][j + i] = a
+                    m = jnp.maximum(m, lane_groups(a, jnp.maximum))
+                m_refs[par][...] = m
+            if 2 in stages:
+                top = wide(m_refs[1 - par][...])
+                l = l_refs[1 - par][...]
+                for i in range(width):
+                    w = jnp.exp2((sc[1 - par][j + i] - top) * scale)
+                    sc[1 - par][j + i] = w
+                    l += lane_groups(w, jnp.add)
+                l_refs[1 - par][...] = l
             return z
 
-        def weights(j, z):
-            for h in range(2):
-                p = jnp.exp2((sc_ref[h, j] - wide(m_ref[h])) * scale)
-                sc_ref[h, j] = p
-                l_ref[h] = l_ref[h] + lane_groups(p, jnp.add)
-            return z
-
-        def values(j, z):
-            k_at = pl.ds(_mo(j, BK), BK)
-            for h in range(2):
-                v = kv_ref[g, k_at, 2 * HEAD_DIM * h + HEAD_DIM : 2 * HEAD_DIM * (h + 1)]
-                p = (sc_ref[h, j] * wide(l_ref[h])).astype(jnp.bfloat16)
-                acc_ref[h] = acc_ref[h] + jnp.dot(p, v, preferred_element_type=jnp.float32)
-            return z
-
-        lax.fori_loop(0, full, functools.partial(scores, diagonal=False), 0)
-        scores(full, 0, True)
-        for h in range(2):
-            m_ref[h] = jnp.broadcast_to(jnp.max(m_ref[h], axis=1, keepdims=True), (BQ, HEAD_DIM))
-        lax.fori_loop(0, full + 1, weights, 0)
-        for h in range(2):
-            l_ref[h] = jnp.broadcast_to(1.0 / jnp.sum(l_ref[h], axis=1, keepdims=True), (BQ, HEAD_DIM))
-        lax.fori_loop(0, full + 1, values, 0)
-        for h in range(2):
-            xg[t, q_at, pl.ds(pl.multiple_of(g * CP + h * HEAD_DIM, HEAD_DIM), HEAD_DIM)] = acc_ref[h].astype(jnp.bfloat16)
+        lax.fori_loop(0, s, lambda i, z: tile(2 * i, z, 2, False), 0)
+        lax.fori_loop(0, half, lambda i, z: tile(2 * s, z, 1, False), 0)
+        tile(full, 0, 1, True)
+        if 1 in stages:
+            m_refs[par][...] = jnp.broadcast_to(jnp.max(m_refs[par][...], axis=1, keepdims=True), (BQ, HEAD_DIM))
+        if 2 in stages:
+            l_refs[1 - par][...] = jnp.broadcast_to(1.0 / jnp.sum(l_refs[1 - par][...], axis=1, keepdims=True), (BQ, HEAD_DIM))
+        if 3 in stages:
+            xg[t, pl.ds(_mo(b3, BQ), BQ), pl.ds(_mo(h3, HEAD_DIM), HEAD_DIM)] = acc_ref[...].astype(jnp.bfloat16)
 
     def dot_rows(panel, out, r):
         acc = jnp.dot(xg[0, rows(r), :], panel[0], preferred_element_type=jnp.float32)
@@ -567,113 +614,116 @@
             acc += jnp.dot(xg[k, rows(r), :], panel[k], preferred_element_type=jnp.float32)
         out[rows(r), :] = acc.astype(jnp.bfloat16)
 
-    def project(lo, hi):
-        def chunk(r, z):
-            dot_rows(wg2, y2, r)
-            dot_rows(wg, y1, r)
-            y_out(r, to_e).start()
-            return z
-
-        lax.fori_loop(lo, hi, chunk, 0)
-
-    def pieces_in(lo, hi):
-        def wait(u, z):
-            piece_in(0, u).wait_recv()
-            piece_in(1, u).wait_recv()
-            return z
-
-        lax.fori_loop(lo, hi, wait, 0)
-
     def relay_piece(u):
         end_piece(u, to_e).wait_recv()
         passed_piece(u).start()
 
-    def relay_w(u):
-        @pl.when(u < NP)
-        def _():
-            w_z(u, to_e).wait_recv()
-            w_out("y2", u).start()
-            w_out("xo2", u).start()
-            w_out("so2", u).start()
-
-        @pl.when(u == NP - 1)
-        def _():
+    def relay_w(i, kind, p):
+        w_in(i, kind, p).wait_recv()
+        if kind == "y":
+            w_out(i, "x", p).start()
+            w_out(i, "sy", p).start()
+        else:
+            w_out(i, "sx", p).start()
+
+    plan = ((1, "y", 6), (1, "x", 11), (0, "y", 21), (0, "x", 26))
+    steps = H * 2 + 2
+
+    def after(half, k):
+        g = half * steps + k
+        for i, kind, base in plan:
+            @pl.when(is_mid & (g >= base) & (g < base + 4 * NP) & ((g - base) % 4 == 0))
+            def _():
+                relay_w(i, kind, (g - base) // 4)
+
+    def finished(u):
+        @pl.when(is_end)
+        def _():
+            end_piece(u, to_m).start()
+
+        @pl.when(is_mid)
+        def _():
+            @pl.when(u >= 1)
+            def _():
+                relay_piece(u - 1)
+
+            own_piece(u).start()
+
+    def kv_here(half, k):
+        @pl.when((half == 0) & (k < H))
+        def _():
+            for owner in range(NT):
+                @pl.when(owner <= s)
+                def _():
+                    kv_copy(k, owner).wait()
+
+    def panel_here(i):
+        w_own(i).wait()
+        w_sib(i, sib).wait_recv()
+        for kind in ("sy", "sx"):
             for p in range(NP):
-                w_out("y1", p).start()
-
-        @pl.when((u >= 1) & (u <= NP))
-        def _():
-            w_in("y2", u - 1).wait_recv()
-            w_out("x2", u - 1).start()
-            w_out("sy2", u - 1).start()
-
-        @pl.when((u >= NP) & (u < 2 * NP))
-        def _():
-            p = u - NP
-            w_in("y1", p).wait_recv()
-            w_out("x1", p).start()
-            w_out("sy1", p).start()
-            w_in("xo2", p).wait_recv()
-            w_out("sx2", p).start()
-
-        @pl.when((u >= 2 * NP) & (u < 3 * NP))
-        def _():
-            p = u - 2 * NP
-            w_in("x2", p).wait_recv()
-            w_out("sxy2", p).start()
-            w_in("x1", p).wait_recv()
-            w_out("sx1", p).start()
-
-        @pl.when(u == 3 * NP - 1)
-        def _():
-            own_w.wait()
-            w_so1_in.wait_recv()
-            for kind in ("so2", "sy2", "sx2", "sxy2", "sy1", "sx1"):
-                for p in range(NP):
-                    w_in(kind, p).wait_recv()
-
-    per = C // CP
-    cb = BQ // RC
-
-    def step(u, z):
-        @pl.when(u < per)
-        def _():
-            for k in range(NT):
-                @pl.when(k <= s)
-                def _():
-                    kv_copy(u, k).wait()
-
-        attend(u)
-
-        @pl.when(is_end)
-        def _():
-            end_piece(u, to_m).start()
-
-        @pl.when(is_mid)
-        def _():
-            relay_w(u)
-
-            @pl.when(u >= 1)
-            def _():
-                relay_piece(u - 1)
-
-            own_piece(u).start()
-
-            @pl.when((u == NU - 5) | (u == NU - 2))
-            def _():
-                late = (u - (NU - 5)) // 3
-                pieces_in(late * 2 * per, 2 * per + late * per)
-                project(late * 2 * cb, 2 * cb + late * cb)
-
+                w_in(i, kind, p).wait_recv()
+
+    def end_columns(b, n):
+        for u in range(n * per):
+            piece_in(0, b * per + u).wait_recv()
+            piece_in(1, b * per + u).wait_recv()
+        lo, hi = b * (BQ // RC), (b + n) * (BQ // RC)
+
+        def chunk(r, z):
+            dot_rows(wg2, y2, r)
+
+            @pl.when(r > lo)
+            def _():
+                y_out(r - 1, to_e).start()
+
+            return z
+
+        lax.fori_loop(lo, hi, chunk, 0)
+
+    def half_rows(half, z):
+        kv_here(half, 0)
+        attend(half, 0, 0, (1,))
+        after(half, 0)
+        kv_here(half, 1)
+        attend(half, 1, 1, (1, 2))
+        after(half, 1)
+
+        def pair(i, z):
+            for par in range(2):
+                k = 2 * i + par
+                kv_here(half, k)
+                attend(half, k, par, (1, 2, 3))
+                after(half, k)
+            finished(half * 2 * per + i - 1)
+
+            @pl.when(is_mid & (half == 1) & (i == 4))
+            def _():
+                panel_here(1)
+                end_columns(0, 2)
+
+            @pl.when(is_mid & (half == 1) & (i == 5))
+            def _():
+                y_out(2 * (BQ // RC) - 1, to_e).start()
+
+            @pl.when(is_mid & (half == 1) & (i == H - 1))
+            def _():
+                end_columns(2, 1)
+
+            return z
+
+        lax.fori_loop(1, H, pair, 0)
+        attend(half, 2 * H, 0, (2, 3))
+        after(half, 2 * H)
+        attend(half, 2 * H + 1, 1, (3,))
+        after(half, 2 * H + 1)
+        finished(half * 2 * per + 2 * per - 1)
         return z
 
-    lax.fori_loop(0, NU, step, 0)
+    lax.fori_loop(0, NB // 2, half_rows, 0)
 
     @pl.when(is_end)
     def _():
-        for p in range(NP):
-            w_z(p, to_m).wait_send()
-
         def drain(u, z):
             end_piece(u, to_m).wait_send()
             return z
@@ -685,11 +735,27 @@
     @pl.when(is_mid)
     def _():
         relay_piece(NU - 1)
-        pieces_in(3 * per, NU)
-        project(3 * cb, NR)
+        for i, kind, base in plan:
+            for p in range(NP):
+                if base + 4 * p >= 2 * steps:
+                    relay_w(i, kind, p)
+
+        y_out(3 * (BQ // RC) - 1, to_e).start()
+        panel_here(0)
+        end_columns(3, 1)
+
+        def own_columns(r, z):
+            dot_rows(wg, y1, r)
+
+            @pl.when(r == 0)
+            def _():
+                y_out(NR - 1, to_e).start()
+
+            return z
+
+        lax.fori_loop(0, NR, own_columns, 0)
         own_y = pltpu.make_async_copy(y1, y_hbm, loc.at[0])
         own_y.start()
-        w_so1.wait_send()
 
         def drain(u, z):
             own_piece(u).wait_send()
@@ -699,13 +765,15 @@
         lax.fori_loop(0, NU, drain, 0)
         for r in range(NR):
             y_out(r, to_e).wait_send()
-        for kind in kinds:
-            for p in range(NP):
-                w_out(kind, p).wait_send()
+        for i in range(2):
+            w_sib(i, s).wait_send()
+            for kind in kinds:
+                for p in range(NP):
+                    w_out(i, kind, p).wait_send()
         own_y.wait()
 
 
-def _attend_call(q, kv_all, seg_all, w):
+def _attend_call(q, kv_all, seg_all, w, w2):
     R, C = q.shape
     N = w.shape[1]
     BQ = R // NB
@@ -713,37 +781,37 @@
     dma = pltpu.SemaphoreType.DMA
     hbm = pl.BlockSpec(memory_space=pltpu.HBM)
     bf16, f32 = jnp.bfloat16, jnp.float32
-    stat = pltpu.VMEM((2, BQ, HEAD_DIM), f32)
+    stat = pltpu.VMEM((BQ, HEAD_DIM), f32)
+    scores = pltpu.VMEM((NT * NB // 2, BQ, 2 * BQ), f32)
     return pl.pallas_call(
         _attend_out,
         out_shape=jax.ShapeDtypeStruct((R, N), bf16),
-        in_specs=[hbm] * 4,
+        in_specs=[hbm] * 5,
         out_specs=hbm,
         scratch_shapes=[
             pltpu.VMEM((R, C), bf16),
-            pltpu.VMEM((C // (2 * HEAD_DIM), NT * R, 4 * HEAD_DIM), bf16),
+            pltpu.VMEM((C // HEAD_DIM, NT * R, 2 * HEAD_DIM), bf16),
             pltpu.VMEM(seg_all.shape, jnp.int32),
             pltpu.VMEM((R, HEAD_DIM), jnp.int32),
-            pltpu.VMEM((2, NT * NB // 2, BQ, 2 * BQ), f32),
-            stat, stat, stat,
+            scores, scores, stat, stat, stat, stat, stat,
             pltpu.VMEM((NT, R, C), bf16),
             pltpu.VMEM((NT, C, N), bf16),
             pltpu.VMEM((NT, C, N), bf16),
             pltpu.VMEM((R, N), bf16),
             pltpu.VMEM((R, N), bf16),
-            dma((5,)), dma((C // (2 * HEAD_DIM), NT)), dma((11, NP)), dma((11, NP)), dma((2, NU)), dma((2, NU)), dma((NU,)), dma((NU,)),
-            dma((NP,)), dma((NP,)), dma((NR,)), dma((NR,)),
+            dma((8,)), dma((C // HEAD_DIM, NT)), dma((2, 4, NP)), dma((2, 4, NP)), dma((2, NU)), dma((2, NU)), dma((NU,)), dma((NU,)),
+            dma((NR,)), dma((NR,)),
         ],
         compiler_params=pltpu.CompilerParams(collective_id=1, has_side_effects=True, vmem_limit_bytes=62 * MIB),
         cost_estimate=pl.CostEstimate(flops=4 * R * NT * C * N, bytes_accessed=2 * NT * (R * C + C * N), transcendentals=R * NT * R * 4),
         name="attend_out",
-    )(q, kv_all, seg_all, w)
+    )(q, kv_all, seg_all, w, w2)
 
 
 def solution(mesh):
     def local_block(x_blk, wqkv_blk, wout_blk, seg_blk):
-        q, kv_all, seg_all = _gather_call(True, x_blk, wqkv_blk, seg_blk.reshape(-1, 128))
-        return _attend_call(q, kv_all, seg_all.reshape(-1, 128), wout_blk)
+        q, kv_all, seg_all, w2 = _gather_call(True, x_blk, wqkv_blk, seg_blk.reshape(-1, 128), wout_blk)
+        return _attend_call(q, kv_all, seg_all.reshape(-1, 128), wout_blk, w2)
 
     row_spec = P(("dp", "sp"), "tp")
     return jax.shard_map(local_block, mesh=mesh, in_specs=(row_spec, P("sp", "tp"), P("sp", "tp"), P(("dp", "sp"))), out_specs=row_spec, check_vma=False)

time: 324 us -> 294 us (0.907)
  Pallas kernels: 320 us -> 291 us
    pallas_call x1, Pallas kernels: 150 us -> 120 us  [_attend_call(): pl.pallas_call(_attend_out, out_shape=jax.ShapeDtypeStruct((R, N), bf16),...]
where the time goes in v4:
time: 294 us
  Pallas kernels  291 us (99%)
  local copies, waits for them, and re-layouts  3.08 us (1%)
    pallas_call x1, Pallas kernels, _gather_call(): pl.pallas_call(functools.partial(_gather_dot, qkv), out_shape=out_shape,...  170 us
    pallas_call x1, Pallas kernels, _attend_call(): pl.pallas_call(_attend_out, out_shape=jax.ShapeDtypeStruct((R, N), bf16),...  120 us

profile of v4, /device:TPU:7, one launch (start us, length us, event | category | flops | bytes accessed | tf_op | source)
XLA Modules:
  0.0 293.7 jit_solution(4201687697837150375)
XLA Ops:
  0.0 170.3 %qkv_dot.1 = (bf16[1024,1024]{1,0:T(8,128)(2,1)}, bf16[4,1024,2048]{2,1,0:T(8,128)(2,1)}, s32[4,8,128]{2,1,0:T(8,128)}, bf16[1024,1024]{1,0:T(8,128)(2,1)}) custom-call(bf16[1024,1024]{1,0:T(8,128)(2,1)} %x_hbm.1, bf16[1024,3072]{1,0:T(8,128)(2,1)} %w_hbm.2, s32[8,128]{1,0:T(8,128)} %bitcast.2, bf16[1024,1024]{1,0:T(8,128)(2,1)} %w_hbm.3), custom_call_target="tpu_custom_call" | custom-call | flops 25769803776 | bytes 33554432 | tf_op jit(solution)/shard_map/qkv_dot/pallas_call | solution.py:401
  170.3 120.4 %attend_out.1 = bf16[1024,1024]{1,0:T(8,128)(2,1)} custom-call(bf16[1024,1024]{1,0:T(8,128)(2,1)} %get-tuple-element.9.q_hbm, bf16[4,1024,2048]{2,1,0:T(8,128)(2,1)} %get-tuple-element.10.kv_hbm, s32[32,128]{1,0:T(8,128)} %bitcast.3, bf16[1024,1024]{1,0:T(8,128)(2,1)} %w_hbm.3, bf16[1024,1024]{1,0:T(8,128)(2,1)} %get-tuple-element.12.w2_hbm), custom_call_target="tpu_custom_call" | custom-call | flops 17179869184 | bytes 16777216 | tf_op jit(solution)/shard_map/attend_out/pallas_call | solution.py:786
  290.6 3.1 %copy.6 = bf16[1024,1024]{1,0:T(8,128)(2,1)} copy(bf16[1024,1024]{1,0:T(8,128)(2,1)} %attend_out.1) | data formatting | bytes 4194304

commit v5 on v4

--- a/solution.py
+++ b/solution.py
@@ -11,6 +11,8 @@
 NT = 4
 NR = 8
 NB = 4
+AHEAD = 2
+LATE = 1
 NP = 4
 LOG2E = 1.4426950408889634
 MIB = 1024 * 1024
@@ -140,12 +142,13 @@
         def _():
             x_own(r, 1).start()
 
-    def relay_x(r):
+    def relay_x(i):
         for dist in range(1, NT):
+            r = i - (dist - 1)
             for way in range(2):
                 here = (t >= dist) if way == 0 else (t <= NT - 1 - dist)
 
-                @pl.when(here)
+                @pl.when(here & (r >= 0) & (r < NR))
                 def _():
                     x_arrive(r, way, dist).wait_recv()
                     if dist < NT - 1:
@@ -153,9 +156,14 @@
                         def _():
                             x_forward(r, way, dist).start()
 
+            if dist == 1:
+                @pl.when(jnp.int32(i + AHEAD) < NR)
+                def _():
+                    send_own_x(i + AHEAD)
+
     own_x = pltpu.make_async_copy(x_hbm, xg.at[t], loc.at[0])
     own_w = pltpu.make_async_copy(w_hbm, wg.at[s], loc.at[1])
-    for r in range(2):
+    for r in range(AHEAD):
         send_own_x(r)
     for p in range(NP):
         w_y(p).start()
@@ -191,6 +199,9 @@
         else:
             y_ref[rows(r), cols] = out
 
+    if qkv:
+        early = kv.shape[1] - LATE * 2 * HEAD_DIM
+
     def kv_cols(p):
         return pl.ds(_mo(p, 4 * HEAD_DIM), 4 * HEAD_DIM)
 
@@ -200,9 +211,15 @@
     def send_unit(r, p):
         pltpu.make_async_copy(kv.at[rows(r), kv_cols(p)], kv_all.at[s, rows(r), kv_cols(p)], loc.at[2]).start()
 
-        @pl.when(yc == 0)
+        @pl.when((yc == 0) & (p < NP - 1))
         def _():
             kv_unit(r, p, to_y, kv_send.at[0], kv_yr.at[r]).start()
+
+        if LATE == 1:
+            @pl.when((yc == 0) & (p == NP - 1))
+            def _():
+                at = pl.ds((NP - 1) * 4 * HEAD_DIM, 2 * HEAD_DIM)
+                remote(kv.at[rows(r), at], kv_all.at[s, rows(r), at], kv_send.at[0], kv_yr.at[r], to_y).start()
 
         @pl.when(c == 0)
         def _():
@@ -212,17 +229,19 @@
         for n, f in work:
             def body(u, z, f=f):
                 unit(*f(u))
+                if qkv:
+                    @pl.when(u > 0)
+                    def _():
+                        send_unit(*f(u - 1))
                 return z
             lax.fori_loop(0, n, body, 0)
-        if qkv:
-            for n, f in work:
-                def body(u, z, f=f):
-                    send_unit(*f(u))
-                    return z
-                lax.fori_loop(0, n, body, 0)
+            if qkv:
+                send_unit(*f(jnp.int32(n - 1)))
 
     def kv_row(r, owner, who, send, recv):
-        return remote(kv_all.at[owner, rows(r)], kv_all.at[owner, rows(r)], send, recv, who)
+        at = pl.ds(0, early if who is not None else kv.shape[1])
+        who = to_sib if who is None else who
+        return remote(kv_all.at[owner, rows(r), at], kv_all.at[owner, rows(r), at], send, recv, who)
 
     def pass_kv(r):
         if qkv:
@@ -270,37 +289,35 @@
             w_f_in(p, 0).wait_recv()
             w_f_in(p, 1).wait_recv()
 
+    LAG = NT - 2
+    relay_x(jnp.int32(0))
     for i in range(NP + 1):
-        relay_x(i)
-        send_own_x(i + 2)
+        relay_x(jnp.int32(i + 1))
         relay_w(i)
         if i == 2:
-            do_units([(6, lambda u: (u // 2, u % 2))])
+            do_units([(4, lambda u: (u // 2, u % 2))])
         if i == 3:
-            do_units([(2, lambda u: (3, u)), (4, lambda u: (u, 2))])
+            do_units([(2, lambda u: (u, 2)), (3, lambda u: (2, u))])
         if i == 4:
-            do_units([(3, lambda u: (4, u)), (5, lambda u: (u, 3))])
+            do_units([(3, lambda u: (u, 3)), (4, lambda u: (3, u))])
 
     def late(i, z):
         relay_x(i)
-
-        @pl.when(i + 2 < NR)
-        def _():
-            send_own_x(i + 2)
-
-        pass_kv(2 * (i - NP - 1))
-        pass_kv(2 * (i - NP - 1) + 1)
-
-        @pl.when(is_mid & (i < NP + 3))
+        @pl.when(i >= NP + 3)
+        def _():
+            pass_kv(2 * (i - NP - 3))
+            pass_kv(2 * (i - NP - 3) + 1)
+
+        @pl.when(is_mid & (i < NP + 4))
         def _():
             for p in range(2):
-                z_in(2 * (i - NP - 1) + p).wait_recv()
-                zx(2 * (i - NP - 1) + p, True).start()
-
-        do_units([(NP, lambda u: (i, u))])
+                z_in(2 * (i - NP - 2) + p).wait_recv()
+                zx(2 * (i - NP - 2) + p, True).start()
+
+        do_units([(NP, lambda u: (i - LAG, u))])
         return z
 
-    lax.fori_loop(NP + 1, NR, late, 0)
+    lax.fori_loop(NP + 2, NR + LAG, late, 0)
 
     for p in range(NP):
         w_own(p).wait_send()
@@ -352,7 +369,8 @@
 
         @pl.when(yc == 0)
         def _():
-            remote(kv, kv_all.at[s], kv_send.at[0], kv_yr.at[0], to_y).wait_send()
+            at = pl.ds(0, early)
+            remote(kv.at[:, at], kv_all.at[s, :, at], kv_send.at[0], kv_yr.at[0], to_y).wait_send()
 
         @pl.when(c == 0)
         def _():
@@ -361,7 +379,7 @@
         def drain_kv(r, z):
             @pl.when(c == 1)
             def _():
-                kv_row(r, sib, to_sib, kv_fs.at[r], kv_cr.at[r]).wait_recv()
+                kv_row(r, sib, None, kv_fs.at[r], kv_cr.at[r]).wait_recv()
 
             @pl.when(yc == 1)
             def _():
@@ -411,11 +429,11 @@
 
 
 def _attend_out(q_hbm, kv_hbm, seg_hbm, w_hbm, w2_hbm, y_hbm, q_ref, kv_ref, seg_ref, first_ref, sc0, sc1, m0, m1, l0, l1, acc_ref, xg, wg, wg2,
-                y1, y2, loc, kv_sem, w_send, w_recv, o_send, o_recv, e_send, e_recv, y_send, y_recv):
+                y1, y2, loc, kv_sem, late_sem, w_send, w_recv, o_send, o_recv, e_send, e_recv, y_send, y_recv):
     R, C = q_hbm.shape
     N = w_hbm.shape[1]
-    RC, NH = R // NR, N // (2 * NP)
     BQ = R // NB
+    NH = N // (2 * NP)
     BK = 2 * BQ
     H = C // HEAD_DIM
     CP = 2 * HEAD_DIM
@@ -439,8 +457,8 @@
     def remote(src, dst, send, recv, who):
         return pltpu.make_async_remote_copy(src, dst, send, recv, device_id=who, device_id_type=mesh_id)
 
-    def rows(r):
-        return pl.ds(_mo(r, RC), RC)
+    def rows(b):
+        return pl.ds(_mo(b, BQ), BQ)
 
     def mine(p):
         return pl.ds(_mo(2 * p + d, NH), NH)
@@ -506,20 +524,43 @@
     q_copy.start()
     for h in range(H):
         for k in range(NT):
-            @pl.when(k <= s)
+            @pl.when((k <= s) & (yc == 0) if h >= H - LATE and k < NT // 2 else k <= s)
             def _():
                 kv_copy(h, k).start()
 
+    greet(to_y)
+    greet(to_sib)
+
     @pl.when(is_end)
     def _():
         greet(to_m)
-        pl.semaphore_wait(bar, 1)
+        pl.semaphore_wait(bar, 3)
 
     @pl.when(is_mid)
     def _():
-        for who in (to_e, to_o, to_y, to_x, to_sib):
+        for who in (to_e, to_o, to_x):
             greet(who)
         pl.semaphore_wait(bar, 5)
+
+    def late_y(i):
+        h = H - LATE + i
+        return remote(kv_hbm.at[s, :, pl.ds(h * CP, CP)], kv_ref.at[h, pl.ds(_mo(s, R), R)], late_sem.at[0, i], late_sem.at[1, i], to_y)
+
+    def late_kv(i, owner):
+        at = kv_ref.at[H - LATE + i, pl.ds(_mo(owner, R), R)]
+        return remote(at, at, late_sem.at[2, i], late_sem.at[3, i], to_sib)
+
+    def late_y_in(i):
+        at = kv_ref.at[H - LATE + i, pl.ds(_mo(ynb, R), R)]
+        return remote(at, at, late_sem.at[0, i], late_sem.at[1, i], to_y)
+
+    @pl.when(yc == 0)
+    def _():
+        for i in range(LATE):
+            late_y(i).start()
+
+    @pl.when(is_mid)
+    def _():
         for i in (1, 0):
             for p in range(NP):
                 w_out(i, "y", p).start()
@@ -631,6 +672,12 @@
 
     def after(half, k):
         g = half * steps + k
+        for i in range(LATE):
+            @pl.when((yc == 1) & (g == H - 2 - LATE + i))
+            def _():
+                late_y_in(i).wait_recv()
+                late_kv(i, ynb).start()
+
         for i, kind, base in plan:
             @pl.when(is_mid & (g >= base) & (g < base + 4 * NP) & ((g - base) % 4 == 0))
             def _():
@@ -653,9 +700,13 @@
         @pl.when((half == 0) & (k < H))
         def _():
             for owner in range(NT):
-                @pl.when(owner <= s)
+                @pl.when((owner <= s) & ((yc == 0) | (k < H - LATE)) if owner < NT // 2 else owner <= s)
                 def _():
                     kv_copy(k, owner).wait()
+            for i in range(LATE):
+                @pl.when((yc == 1) & (k == H - LATE + i))
+                def _():
+                    late_kv(i, diag).wait_recv()
 
     def panel_here(i):
         w_own(i).wait()
@@ -668,18 +719,16 @@
         for u in range(n * per):
             piece_in(0, b * per + u).wait_recv()
             piece_in(1, b * per + u).wait_recv()
-        lo, hi = b * (BQ // RC), (b + n) * (BQ // RC)
-
         def chunk(r, z):
             dot_rows(wg2, y2, r)
 
-            @pl.when(r > lo)
+            @pl.when(r > b)
             def _():
                 y_out(r - 1, to_e).start()
 
             return z
 
-        lax.fori_loop(lo, hi, chunk, 0)
+        lax.fori_loop(b, b + n, chunk, 0)
 
     def half_rows(half, z):
         kv_here(half, 0)
@@ -704,7 +753,7 @@
 
             @pl.when(is_mid & (half == 1) & (i == 5))
             def _():
-                y_out(2 * (BQ // RC) - 1, to_e).start()
+                y_out(1, to_e).start()
 
             @pl.when(is_mid & (half == 1) & (i == H - 1))
             def _():
@@ -715,12 +764,25 @@
         lax.fori_loop(1, H, pair, 0)
         attend(half, 2 * H, 0, (2, 3))
         after(half, 2 * H)
+
+        @pl.when(is_mid & (half == 1))
+        def _():
+            y_out(2, to_e).start()
+
         attend(half, 2 * H + 1, 1, (3,))
         after(half, 2 * H + 1)
         finished(half * 2 * per + 2 * per - 1)
         return z
 
     lax.fori_loop(0, NB // 2, half_rows, 0)
+    for i in range(LATE):
+        @pl.when(yc == 0)
+        def _():
+            late_y(i).wait_send()
+
+        @pl.when(yc == 1)
+        def _():
+            late_kv(i, ynb).wait_send()
 
     @pl.when(is_end)
     def _():
@@ -729,7 +791,7 @@
             return z
 
         lax.fori_loop(0, NU, drain, 0)
-        for r in range(NR):
+        for r in range(NB):
             y_out(r, to_m).wait_recv()
 
     @pl.when(is_mid)
@@ -740,20 +802,15 @@
                 if base + 4 * p >= 2 * steps:
                     relay_w(i, kind, p)
 
-        y_out(3 * (BQ // RC) - 1, to_e).start()
+        end_columns(3, 1)
         panel_here(0)
-        end_columns(3, 1)
+        y_out(NB - 1, to_e).start()
 
         def own_columns(r, z):
             dot_rows(wg, y1, r)
-
-            @pl.when(r == 0)
-            def _():
-                y_out(NR - 1, to_e).start()
-
             return z
 
-        lax.fori_loop(0, NR, own_columns, 0)
+        lax.fori_loop(0, NB, own_columns, 0)
         own_y = pltpu.make_async_copy(y1, y_hbm, loc.at[0])
         own_y.start()
 
@@ -763,7 +820,7 @@
             return z
 
         lax.fori_loop(0, NU, drain, 0)
-        for r in range(NR):
+        for r in range(NB):
             y_out(r, to_e).wait_send()
         for i in range(2):
             w_sib(i, s).wait_send()
@@ -799,8 +856,8 @@
             pltpu.VMEM((NT, C, N), bf16),
             pltpu.VMEM((R, N), bf16),
             pltpu.VMEM((R, N), bf16),
-            dma((8,)), dma((C // HEAD_DIM, NT)), dma((2, 4, NP)), dma((2, 4, NP)), dma((2, NU)), dma((2, NU)), dma((NU,)), dma((NU,)),
-            dma((NR,)), dma((NR,)),
+            dma((8,)), dma((C // HEAD_DIM, NT)), dma((4, LATE)), dma((2, 4, NP)), dma((2, 4, NP)), dma((2, NU)), dma((2, NU)), dma((NU,)), dma((NU,)),
+            dma((NB,)), dma((NB,)),
         ],
         compiler_params=pltpu.CompilerParams(collective_id=1, has_side_effects=True, vmem_limit_bytes=62 * MIB),
         cost_estimate=pl.CostEstimate(flops=4 * R * NT * C * N, bytes_accessed=2 * NT * (R * C + C * N), transcendentals=R * NT * R * 4),

time: 294 us -> 286 us (0.973)
  Pallas kernels: 291 us -> 283 us
    pallas_call x1, Pallas kernels: 170 us -> 161 us  [_gather_call(): pl.pallas_call(functools.partial(_gather_dot, qkv), out_shape=out_shape,...]
where the time goes in v5:
time: 286 us
  Pallas kernels  283 us (99%)
  local copies, waits for them, and re-layouts  3.08 us (1%)
    pallas_call x1, Pallas kernels, _gather_call(): pl.pallas_call(functools.partial(_gather_dot, qkv), out_shape=out_shape,...  161 us
    pallas_call x1, Pallas kernels, _attend_call(): pl.pallas_call(_attend_out, out_shape=jax.ShapeDtypeStruct((R, N), bf16),...  122 us

profile of v5, /device:TPU:7, one launch (start us, length us, event | category | flops | bytes accessed | tf_op | source)
XLA Modules:
  0.0 285.8 jit_solution(5760540144146620137)
XLA Ops:
  0.0 160.9 %qkv_dot.1 = (bf16[1024,1024]{1,0:T(8,128)(2,1)}, bf16[4,1024,2048]{2,1,0:T(8,128)(2,1)}, s32[4,8,128]{2,1,0:T(8,128)}, bf16[1024,1024]{1,0:T(8,128)(2,1)}) custom-call(bf16[1024,1024]{1,0:T(8,128)(2,1)} %x_hbm.1, bf16[1024,3072]{1,0:T(8,128)(2,1)} %w_hbm.2, s32[8,128]{1,0:T(8,128)} %bitcast.2, bf16[1024,1024]{1,0:T(8,128)(2,1)} %w_hbm.3), custom_call_target="tpu_custom_call" | custom-call | flops 25769803776 | bytes 33554432 | tf_op jit(solution)/shard_map/qkv_dot/pallas_call | solution.py:419
  160.9 121.8 %attend_out.1 = bf16[1024,1024]{1,0:T(8,128)(2,1)} custom-call(bf16[1024,1024]{1,0:T(8,128)(2,1)} %get-tuple-element.9.q_hbm, bf16[4,1024,2048]{2,1,0:T(8,128)(2,1)} %get-tuple-element.10.kv_hbm, s32[32,128]{1,0:T(8,128)} %bitcast.3, bf16[1024,1024]{1,0:T(8,128)(2,1)} %w_hbm.3, bf16[1024,1024]{1,0:T(8,128)(2,1)} %get-tuple-element.12.w2_hbm), custom_call_target="tpu_custom_call" | custom-call | flops 17179869184 | bytes 16777216 | tf_op jit(solution)/shard_map/attend_out/pallas_call | solution.py:843
  282.7 3.1 %copy.6 = bf16[1024,1024]{1,0:T(8,128)(2,1)} copy(bf16[1024,1024]{1,0:T(8,128)(2,1)} %attend_out.1) | data formatting | bytes 4194304

commit v6 on v5

--- a/solution.py
+++ b/solution.py
@@ -11,7 +11,7 @@
 NT = 4
 NR = 8
 NB = 4
-AHEAD = 2
+AHEAD = 1
 LATE = 1
 NP = 4
 LOG2E = 1.4426950408889634

time: 286 us -> 286 us (level)
  no operation moved by 1% of the time
where the time goes in v6:
time: 286 us; the launch traced here: 285 us
  Pallas kernels  282 us (99%)
  local copies, waits for them, and re-layouts  3.08 us (1%)
    pallas_call x1, Pallas kernels, _gather_call(): pl.pallas_call(functools.partial(_gather_dot, qkv), out_shape=out_shape,...  163 us
    pallas_call x1, Pallas kernels, _attend_call(): pl.pallas_call(_attend_out, out_shape=jax.ShapeDtypeStruct((R, N), bf16),...  119 us

profile of v6, /device:TPU:7, one launch (start us, length us, event | category | flops | bytes accessed | tf_op | source)
XLA Modules:
  0.0 285.1 jit_solution(13225279853042723770)
XLA Ops:
  0.0 162.9 %qkv_dot.1 = (bf16[1024,1024]{1,0:T(8,128)(2,1)}, bf16[4,1024,2048]{2,1,0:T(8,128)(2,1)}, s32[4,8,128]{2,1,0:T(8,128)}, bf16[1024,1024]{1,0:T(8,128)(2,1)}) custom-call(bf16[1024,1024]{1,0:T(8,128)(2,1)} %x_hbm.1, bf16[1024,3072]{1,0:T(8,128)(2,1)} %w_hbm.2, s32[8,128]{1,0:T(8,128)} %bitcast.2, bf16[1024,1024]{1,0:T(8,128)(2,1)} %w_hbm.3), custom_call_target="tpu_custom_call" | custom-call | flops 25769803776 | bytes 33554432 | tf_op jit(solution)/shard_map/qkv_dot/pallas_call | solution.py:419
  162.9 119.2 %attend_out.1 = bf16[1024,1024]{1,0:T(8,128)(2,1)} custom-call(bf16[1024,1024]{1,0:T(8,128)(2,1)} %get-tuple-element.9.q_hbm, bf16[4,1024,2048]{2,1,0:T(8,128)(2,1)} %get-tuple-element.10.kv_hbm, s32[32,128]{1,0:T(8,128)} %bitcast.3, bf16[1024,1024]{1,0:T(8,128)(2,1)} %w_hbm.3, bf16[1024,1024]{1,0:T(8,128)(2,1)} %get-tuple-element.12.w2_hbm), custom_call_target="tpu_custom_call" | custom-call | flops 17179869184 | bytes 16777216 | tf_op jit(solution)/shard_map/attend_out/pallas_call | solution.py:843
  282.0 3.1 %copy.6 = bf16[1024,1024]{1,0:T(8,128)(2,1)} copy(bf16[1024,1024]{1,0:T(8,128)(2,1)} %attend_out.1) | data formatting | bytes 4194304
